TPU v7x, 32 devices: a whole 2x2x4 slice. The times are simulated.
32 devices in a mesh: seq: 16 (over z, y, x), tp: 2 (over core).
Axes of the slice: x: 2, y: 2, z: 4, core: 2. Of those that a mesh axis runs over, the one named last changes fastest.
Arguments:
- inner_input: bfloat16 [4096, 2560], P('seq', 'tp'), may hold values from -6 to 6
- gate_input: bfloat16 [4096, 2560], P('seq', 'tp'), may hold values from -170 to 170
- state_input: bfloat16 [4096, 256], P('seq'), may hold values from -6 to 6
- step_raw: float32 [40, 4096], P('tp', 'seq'), may hold values from -14 to 0
- conv_inner: float32 [4, 2560], P(None, 'tp'), may hold values from -3 to 3
- conv_state: float32 [4, 256], replicated, may hold values from -3 to 3
- bias_inner: float32 [2560], P('tp'), may hold values from -3 to 3
- bias_state: float32 [256], replicated, may hold values from -3 to 3
- step_bias: float32 [40], P('tp'), may hold values from -0.3 to 0.3
- decay_log: float32 [40], P('tp'), may hold values from -1.4 to 0
- skip_gain: float32 [40], P('tp'), may hold values from 0.5 to 1.5
- norm_gain: float32 [2560], P('tp'), may hold values from 0.1 to 1.9
- out_weight: bfloat16 [2560, 2560], P('tp'), may hold values from -0.15625 to 0.15625
Outputs:
- block_out: bfloat16 [4096, 2560], P('seq', 'tp')
All inputs are finite; a program needn't handle non-finite values.
Results may differ from a plain program's by a relative error of at most 0.008.
Values may be sent and summed in bfloat16 or wider, within the bound.
No kernel may reach another device: no remote copies, remote signals or barrier semaphores. Data moves between devices by JAX's collectives and lax.ppermute only.
A program may use at most 64 MiB of HBM per device.

v0:
```python
import jax
import jax.numpy as jnp
from jax import lax
from jax.sharding import PartitionSpec as P

HEAD_DIM = 64
NSTATE = 128
INNER = 2560


highest = lax.Precision.HIGHEST


def passed_along(value, axis, steps):
    count = lax.axis_size(axis)
    leading, last = (max(0, -steps), min(count, count - steps))
    return lax.ppermute(value, axis, [(source, source + steps) for source in range(leading, last)])


def conv_silu(padded, weights, offsets, length):
    width_taps = weights.shape[0]
    summed = offsets[None, :] + jnp.zeros((length, weights.shape[1]), jnp.float32)
    for number in range(width_taps):
        summed = summed + weights[number][None, :] * padded[number : number + length]
    return jax.nn.silu(summed).astype(jnp.bfloat16)


def block_pass(inner_rows, keys_b, query_c, step_sizes, log_decay, state_now):
    cumulative = jnp.cumsum(log_decay, axis=1)
    block_rows = log_decay.shape[1]
    causal = jnp.arange(block_rows)[:, None] >= jnp.arange(block_rows)[None, :]
    spread = jnp.where(causal[None], cumulative[:, :, None] - cumulative[:, None, :], -jnp.inf)
    scores = jnp.dot(query_c, keys_b.T, preferred_element_type=jnp.float32)
    weights = scores[None] * jnp.exp(spread) * step_sizes[:, None, :]
    output = jnp.einsum("hts,shp->thp", weights, inner_rows, precision=highest)
    query_float = query_c.astype(jnp.float32)
    carried = jnp.einsum("tn,hnp->thp", query_float, state_now, precision=highest)
    output = output + carried * jnp.exp(cumulative).T[:, :, None]
    towards_end = jnp.exp(cumulative[:, -1:] - cumulative) * step_sizes
    update = jnp.einsum(
        "sn,shp->hnp",
        keys_b.astype(jnp.float32),
        inner_rows * towards_end.T[:, :, None],
        precision=highest,
    )
    state_next = jnp.exp(cumulative[:, -1])[:, None, None] * state_now + update
    return (state_next, output)


def combine_rows(earlier, later):
    return (earlier[0] * later[0], later[0][..., None] * earlier[1] + later[1])


def local(
    inner_input,
    gate_input,
    state_input,
    step_raw,
    conv_inner,
    conv_state,
    bias_inner,
    bias_state,
    step_bias,
    decay_log,
    skip_gain,
    norm_gain,
    out_weight,
):
    width_taps = conv_inner.shape[0]
    tok_rows = inner_input.shape[0]
    head_count = step_raw.shape[0]
    rims = passed_along(
        (inner_input[tok_rows - width_taps + 1 :], state_input[tok_rows - width_taps + 1 :]),
        "seq",
        1,
    )
    inner_conv = conv_silu(
        jnp.concatenate([rims[0], inner_input], axis=0).astype(jnp.float32),
        conv_inner,
        bias_inner,
        tok_rows,
    )
    state_conv = conv_silu(
        jnp.concatenate([rims[1], state_input], axis=0).astype(jnp.float32),
        conv_state,
        bias_state,
        tok_rows,
    )
    step_sizes = jax.nn.softplus(step_raw + step_bias[:, None])
    log_decay = -jnp.exp(decay_log)[:, None] * step_sizes
    inner_float = inner_conv.astype(jnp.float32).reshape(tok_rows, head_count, HEAD_DIM)
    keys_b = state_conv[:, :NSTATE]
    query_c = state_conv[:, NSTATE:]
    state_now = jnp.zeros((head_count, NSTATE, HEAD_DIM), jnp.float32)
    state_now, output = block_pass(inner_float, keys_b, query_c, step_sizes, log_decay, state_now)
    device_decay = jnp.exp(jnp.sum(log_decay, axis=1))
    devices = lax.axis_size("seq")
    slice_cols = NSTATE * HEAD_DIM // devices
    sliced = state_now.reshape(head_count, devices, slice_cols)
    received = lax.all_to_all(sliced, "seq", split_axis=1, concat_axis=1, tiled=True)
    all_decays = lax.all_gather(device_decay[None, :], "seq", axis=0, tiled=True)
    by_source = jnp.transpose(received, (1, 0, 2))
    running_prefix = lax.associative_scan(combine_rows, (all_decays, by_source), axis=0)
    exclusive = jnp.concatenate([jnp.zeros_like(by_source[:1]), running_prefix[1][:-1]], axis=0)
    returned = lax.all_to_all(
        jnp.transpose(exclusive, (1, 0, 2)), "seq", split_axis=1, concat_axis=1, tiled=True
    )
    entering_state = returned.reshape(head_count, NSTATE, HEAD_DIM)
    cumulative = jnp.cumsum(log_decay, axis=1)
    carried = jnp.einsum(
        "tn,hnp->thp", query_c.astype(jnp.float32), entering_state, precision=highest
    )
    mixed = (
        output
        + carried * jnp.exp(cumulative).T[:, :, None]
        + skip_gain[None, :, None] * inner_float
    )
    gated_raw = mixed.reshape(tok_rows, head_count * HEAD_DIM) * jax.nn.silu(
        gate_input.astype(jnp.float32)
    )
    local_squares = jnp.sum(gated_raw * gated_raw, axis=1)
    gated = (gated_raw * norm_gain[None, :]).astype(jnp.bfloat16)
    partial_out = jnp.dot(gated, out_weight, preferred_element_type=jnp.float32)
    squares = lax.psum(local_squares, "tp")
    summed = lax.psum_scatter(partial_out, "tp", scatter_dimension=1, tiled=True)
    scale_inv = lax.rsqrt(squares / INNER + 1e-05)
    return (summed * scale_inv[:, None]).astype(jnp.bfloat16)


def solution(mesh):
    return jax.shard_map(
        local,
        mesh=mesh,
        in_specs=(
            P("seq", "tp"),
            P("seq", "tp"),
            P("seq", None),
            P("tp", "seq"),
            P(None, "tp"),
            P(),
            P("tp"),
            P(),
            P("tp"),
            P("tp"),
            P("tp"),
            P("tp"),
            P("tp", None),
        ),
        out_specs=P("seq", "tp"),
        check_vma=False,
    )
```

profile of v0, /device:TPU:0, one launch (start us, length us, event | category | flops | bytes accessed | tf_op | source)
XLA Modules:
  0.0 130.9 jit_solution(17599040376568187160)
XLA Ops:
  6.5 0.8 slice.170
  7.3 4.9 %collective-permute-start.1 = (bf16[3,256]{1,0:T(4,128)(2,1)S(1)}, bf16[3,256]{1,0:T(4,128)(2,1)S(1)}, u32[]{:S(2)}, u32[]{:S(2)}) collective-permute-start(bf16[3,256]{1,0:T(4,128)(2,1)S(1)} %slice.170), channel_id=1, source_target_pairs={{0,2},{2,4},{4,6},{6,8},{8,10},{10,12},{12,14},{14,16},{16,18},{18... | collective-permute-start | bytes 4616 | tf_op jit(solution)/shard_map/ppermute | solution.py:17
  12.2 0.7 slice.161
  12.9 3.4 %collective-permute-start = (bf16[3,1280]{1,0:T(4,128)(2,1)S(1)}, bf16[3,1280]{1,0:T(4,128)(2,1)S(1)}, u32[]{:S(2)}, u32[]{:S(2)}) collective-permute-start(bf16[3,1280]{1,0:T(4,128)(2,1)S(1)} %slice.161), channel_id=1, source_target_pairs={{0,2},{2,4},{4,6},{6,8},{8,10},{10,12},{12,14},{14,16},{16,18},{18... | collective-permute-start | bytes 23048 | tf_op jit(solution)/shard_map/ppermute | solution.py:17
  16.3 0.7 exponential_negate_fusion
  17.0 0.8 fusion.63
  17.8 0.9 fusion.60
  18.8 0.6 reduce-window.6
  19.4 0.2 slice_reduce_fusion
  19.7 0.2 slice_reduce_fusion.1
  20.0 0.9 slice_reduce_fusion.5
  20.9 0.9 maximum_convert_fusion.1
  21.9 0.9 multiply_convert_fusion.4
  22.8 0.1 maximum_convert_fusion
  22.9 0.8 multiply_convert_fusion.2
  23.8 0.2 copy.33
  24.0 0.8 fusion.34
  24.8 0.4 copy.36
  25.2 0.3 reshape.101
  25.6 1.3 copy.37
  26.8 5.9 %all-to-all-start = ((f32[20,16,512]{2,0,1:T(8,128)}), f32[20,16,512]{2,0,1:T(8,128)S(1)}, u32[]{:S(2)}, u32[]{:S(2)}) async-start(f32[20,16,512]{2,0,1:T(8,128)} %copy.37), calls=%async_computation | async-start | bytes 1572864 | tf_op jit(solution)/shard_map/all_to_all | solution.py:100
  32.8 0.6 dynamic-slice
  34.0 0.1 exponential_dynamic-update-slice_fusion
  34.1 45.1 %all-reduce.9 = f32[320]{0:T(512)S(1)} all-reduce(f32[320]{0:T(512)S(1)} %exponential_dynamic-update-slice_fusion), channel_id=2, replica_groups=mesh['seq'=16,'tp'=2] {'seq'}, use_global_device_ids=true, to_apply=%add.9 | all-reduce | flops 320 | bytes 2560
  79.5 0.1 slice_add_fusion
  80.4 0.1 fusion.38
  80.6 0.1 pad.45
  80.7 0.1 pad.70
  80.8 0.1 slice_add_fusion.4
  80.9 1.0 pad_bitcast_fusion
  81.9 3.6 %all-to-all-start.1 = ((f32[20,16,512]{2,0,1:T(8,128)}), f32[20,16,512]{2,0,1:T(8,128)S(1)}, u32[]{:S(2)}, u32[]{:S(2)}) async-start(f32[20,16,512]{2,0,1:T(8,128)} %pad_bitcast_fusion), calls=%async_computation.1 | async-start | bytes 1572864 | tf_op jit(solution)/shard_map/all_to_all | solution.py:105
  85.5 0.2 reduce-scatter.2.cloned.1.call-start
  85.8 0.9 fusion.48
  86.7 1.7 %fusion.39 = f32[256,1280]{0,1} fusion(bf16[256,256]{1,0:T(8,128)(2,1)S(1)} %multiply_convert_fusion.4), kind=kOutput, calls=%fused_computation.48 | convolution fusion | flops 503316480 | bytes 1376256
  88.4 10.3 %all-to-all-done.1 = f32[20,16,512]{2,0,1:T(8,128)S(1)} async-done(((f32[20,16,512]{2,0,1:T(8,128)}), f32[20,16,512]{2,0,1:T(8,128)S(1)}, u32[]{:S(2)}, u32[]{:S(2)}) %all-to-all-start.1) | async-done | bytes 655392 | tf_op jit(solution)/shard_map/all_to_all | solution.py:105
  98.8 0.4 copy.38
  99.1 0.3 reshape.102
  99.4 0.4 copy.39
  99.8 0.7 fusion.50
  100.5 0.6 copy-done
  101.1 4.0 %fusion.21 = f32[256,20,64]{0,2,1:T(8,128)S(1)} fusion(bf16[256,20,64]{0,2,1:T(8,128)(2,1)S(1)} %bitcast.47, f32[20,256]{1,0:T(8,128)S(1)} %get-tuple-element.11, f32[20,256]{1,0:T(8,128)S(1)} %bitcast.54, f32[256,256]{1,0:T(8,128)S(1)} %copy-done.3, pred[256,256]{1,0:T(8,128)(4,1)S(1)} %iota_compare_fusion, f32[256,20,64]{0,2,1:T(8,128)S(1)} %bitcast.51, ...), kind=kOutput, calls=%fused_computation.19 | convolution fusion | flops 1014169600 | bytes 4976720 | tf_op jit(solution)/shard_map/hts,shp->thp/dot_general | solution.py:35
  105.2 0.4 copy.40
  105.6 0.7 copy-done.2
  106.3 6.3 %fusion.35 = f32[256,2560]{1,0:T(8,128)} fusion(bf16[1280,2560]{1,0:T(8,128)(2,1)} %param.25, f32[1280]{0:T(1024)S(1)} %copy-done.5, f32[256,1280]{1,0:T(8,128)S(1)} %copy.40, bf16[256,1280]{1,0:T(8,128)(2,1)S(1)} %copy-done.2), kind=kOutput, calls=%fused_computation.41 | convolution fusion | flops 1680343040 | bytes 11146240 | tf_op jit(solution)/shard_map/dot_general | solution.py:123
  112.6 0.5 multiply_reduce_fusion
  113.1 2.5 %psum.7 = f32[256]{0:T(256)S(1)} all-reduce(f32[256]{0:T(256)S(1)} %multiply_reduce_fusion), channel_id=1, replica_groups=mesh['seq'=16,'tp'=2] {'tp'}, use_global_device_ids=true, to_apply=%region_5.6 | all-reduce | flops 256 | bytes 2048 | tf_op jit(solution)/shard_map/psum | solution.py:124
  115.6 6.2 %reduce-scatter.2.cloned.1.call-done = f32[256,1280]{1,0:T(8,128)} async-done(((f32[256,2560]{1,0:T(8,128)}), f32[256,1280]{1,0:T(8,128)}) %reduce-scatter.2.cloned.1.call-update) | async-done | bytes 1310736 | tf_op jit(solution)/shard_map/reduce_scatter | solution.py:125
  121.8 2.3 %multiply_convert_fusion = bf16[256,1280]{1,0:T(8,128)(2,1)} fusion(f32[256,1280]{1,0:T(8,128)} %reduce-scatter.2.cloned.1.call-done, f32[256]{0:T(256)S(1)} %add_rsqrt_fusion), kind=kLoop, calls=%fused_computation.33 | loop fusion | flops 655360 | bytes 1967104 | tf_op jit(solution)/shard_map/convert_element_type | solution.py:127
  (62 shorter events, 1.4 us)
Async XLA Ops:
  6.5 16.2 %copy-start.1 = (bf16[256,1280]{1,0:T(8,128)(2,1)S(1)}, bf16[256,1280]{1,0:T(8,128)(2,1)}, u32[]{:S(2)}) copy-start(bf16[256,1280]{1,0:T(8,128)(2,1)} %param.13) | copy-start | bytes 1966084
  7.3 13.6 %collective-permute-start.1 = (bf16[3,256]{1,0:T(4,128)(2,1)S(1)}, bf16[3,256]{1,0:T(4,128)(2,1)S(1)}, u32[]{:S(2)}, u32[]{:S(2)}) collective-permute-start(bf16[3,256]{1,0:T(4,128)(2,1)S(1)} %slice.170), channel_id=1, source_target_pairs={{0,2},{2,4},{4,6},{6,8},{8,10},{10,12},{12,14},{14,16},{16,18},{18... | collective-permute-start | bytes 4616 | tf_op jit(solution)/shard_map/ppermute | solution.py:17
  12.9 9.9 %collective-permute-start = (bf16[3,1280]{1,0:T(4,128)(2,1)S(1)}, bf16[3,1280]{1,0:T(4,128)(2,1)S(1)}, u32[]{:S(2)}, u32[]{:S(2)}) collective-permute-start(bf16[3,1280]{1,0:T(4,128)(2,1)S(1)} %slice.161), channel_id=1, source_target_pairs={{0,2},{2,4},{4,6},{6,8},{8,10},{10,12},{12,14},{14,16},{16,18},{18... | collective-permute-start | bytes 23048 | tf_op jit(solution)/shard_map/ppermute | solution.py:17
  21.9 1.0 copy-start.4
  25.6 7.2 %copy-start.7 = (u32[32]{0:T(128)S(1)}, u32[32]{0:T(128)}, u32[]{:S(2)}) copy-start(u32[32]{0:T(128)} %constant.43) | copy-start | bytes 388
  26.8 52.7 %all-to-all-start = ((f32[20,16,512]{2,0,1:T(8,128)}), f32[20,16,512]{2,0,1:T(8,128)S(1)}, u32[]{:S(2)}, u32[]{:S(2)}) async-start(f32[20,16,512]{2,0,1:T(8,128)} %copy.37), calls=%async_computation | async-start | bytes 1572864 | tf_op jit(solution)/shard_map/all_to_all | solution.py:100
  81.9 16.8 %all-to-all-start.1 = ((f32[20,16,512]{2,0,1:T(8,128)}), f32[20,16,512]{2,0,1:T(8,128)S(1)}, u32[]{:S(2)}, u32[]{:S(2)}) async-start(f32[20,16,512]{2,0,1:T(8,128)} %pad_bitcast_fusion), calls=%async_computation.1 | async-start | bytes 1572864 | tf_op jit(solution)/shard_map/all_to_all | solution.py:105
  85.5 36.2 %reduce-scatter.2.cloned.1.call-start = ((), (), s32[]{:S(2)}) async-start(), calls=%async_computation.3 | async-start | bytes 3932160 | tf_op jit(solution)/shard_map/reduce_scatter | solution.py:125
  99.8 1.3 %copy-start = (f32[256,1280]{0,1:S(1)}, f32[256,1280]{0,1}, u32[]{:S(2)}) copy-start(f32[256,1280]{0,1} %fusion.39) | copy-start | bytes 3932164
  99.8 1.3 %copy-start.3 = (f32[256,256]{1,0:T(8,128)S(1)}, f32[256,256]{1,0:T(8,128)}, u32[]{:S(2)}) copy-start(f32[256,256]{1,0:T(8,128)} %fusion.48) | copy-start | bytes 786436
  99.8 1.3 %copy-start.6 = (f32[20]{0:T(128)S(1)}, f32[20]{0:T(128)}, u32[]{:S(2)}) copy-start(f32[20]{0:T(128)} %param.23) | copy-start | bytes 244
  105.2 1.1 copy-start.2
  105.2 1.1 copy-start.5
Sparse Core Ops, SparseCore 0:
  112.7 9.0 reduce-scatter.1
where the time goes:
time: 132 us; the launch traced here: 131 us
  blocking collectives  47.6 us (36%)
  starting transfers between devices  18 us (14%)
  waiting for transfers between devices  16.5 us (12%)
  between operations  14.5 us (11%)
  matrix products  14.4 us (11%)
  local copies, waits for them, and re-layouts  11 us (8%)
  other arithmetic  8.9 us (7%)
    unnamed x1, blocking collectives  45.1 us
    all_to_all x1, waiting for transfers between devices, local(): lax.all_to_all(jnp.transpose(exclusive, (1, 0, 2)), 'seq', split_axis=1,...  10.3 us
    ppermute x2, starting transfers between devices, passed_along(): lax.ppermute(value, axis, [(source, source + steps) for source in range(l...  8.25 us
    dot_general x1, matrix products, local(): partial_out = jnp.dot(gated, out_weight, preferred_element_type=jnp.float32)  6.31 us
    reduce_scatter x1, waiting for transfers between devices, local(): lax.psum_scatter(partial_out, 'tp', scatter_dimension=1, tiled=True)  6.21 us
    all_to_all x1, starting transfers between devices, local(): lax.all_to_all(sliced, 'seq', split_axis=1, concat_axis=1, tiled=True)  5.91 us
    dot_general x1, matrix products, block_pass(): output = jnp.einsum('hts,shp->thp', weights, inner_rows, precision=highest)  4.03 us
    all_to_all x1, starting transfers between devices, local(): lax.all_to_all(jnp.transpose(exclusive, (1, 0, 2)), 'seq', split_axis=1,...  3.61 us
  transfers between devices with their start and end apart: 5, of which 2 were waited for; matrix products, arithmetic and copies ran while one was open for 9% of the time, Pallas kernels for 0%

commit v1 on v0

v1 whole, which is shorter than its diff:
```python
import functools
import jax
import jax.numpy as jnp
from jax import lax
from jax.experimental import pallas as pl
from jax.experimental.pallas import tpu as pltpu
from jax.sharding import PartitionSpec as P

HEAD_DIM = 64
SPREAD = 64
LANES = 128
LOG2E = 1.4426950408889634
highest = lax.Precision.HIGHEST
f32 = jnp.float32
bf16 = jnp.bfloat16


def dot(a, b, contract, precision=None):
    return lax.dot_general(
        a, b, (contract, ((), ())), precision=precision, preferred_element_type=f32
    )


def silu(v):
    return v / (1.0 + jnp.exp(-v))


def spread_matrix(width):
    rows = lax.broadcasted_iota(jnp.int32, (2 * SPREAD, width), 0) & (SPREAD - 1)
    heads = lax.broadcasted_iota(jnp.int32, (2 * SPREAD, width), 1) >> (HEAD_DIM.bit_length() - 1)
    return jnp.where(rows == heads, 1.0, 0.0).astype(bf16)


def split_rows(ref, value):
    heads = value.shape[0]
    high = value.astype(bf16).astype(f32)
    ref[...] = jnp.zeros_like(ref)
    ref[0:heads, :] = high
    ref[SPREAD : SPREAD + heads, :] = value - high
    return ref[...].astype(bf16)


def steps(raw_ref, step_bias_ref, decay_ref):
    v = raw_ref[...] + step_bias_ref[...]
    x = jnp.exp(-jnp.abs(v))
    series = x * (1.0 - x * (0.5 - x * (1.0 / 3.0 - x * 0.25)))
    size = jnp.maximum(v, 0.0) + jnp.where(x < 0.01, series, jnp.log(1.0 + x))
    return size, -jnp.exp(decay_ref[...]) * size


def lower(rows):
    t = lax.broadcasted_iota(jnp.int32, (rows, rows), 0)
    s = lax.broadcasted_iota(jnp.int32, (rows, rows), 1)
    return jnp.where(t >= s, 1.0, 0.0).astype(f32)


def conv_block(scratch, taps_ref, bias_ref, cols, rows):
    taps = taps_ref.shape[0]
    first = 8 - (taps - 1)
    total = jnp.broadcast_to(bias_ref[:, cols], (rows, bias_ref[:, cols].shape[1]))
    for number in range(taps):
        total = total + taps_ref[number : number + 1, cols] * scratch[
            pl.ds(first + number, rows), cols
        ]
    return silu(total)


def update_kernel(
    inner_ref, state_ref, halo_ref, raw_ref, step_bias_ref, decay_ref,
    taps_ref, bias_ref, state_taps_ref, state_bias_ref,
    x_ref, bc_ref, payload_ref, pad, state_pad, parts,
):
    rows, width = inner_ref.shape
    states = state_ref.shape[1]
    half = states // 2
    state_pad[0:8, :] = halo_ref[:, width:].astype(f32)
    state_pad[8:, :] = state_ref[...].astype(f32)
    bc_ref[...] = conv_block(state_pad, state_taps_ref, state_bias_ref, slice(0, states), rows).astype(bf16)
    keys = bc_ref[:, :half]
    size, decay = steps(raw_ref, step_bias_ref, decay_ref)
    cum = dot(decay, lower(rows), ((1,), (1,)), highest)
    weight = jnp.exp(cum[:, rows - 1 :] - cum) * size
    weight = split_rows(parts, weight)
    spread = spread_matrix(width)
    pad[0:8, :] = halo_ref[:, :width].astype(f32)
    pad[8:, :] = inner_ref[...].astype(f32)
    block = 256
    for start in range(0, width, block):
        cols = slice(start, start + block)
        value = conv_block(pad, taps_ref, bias_ref, cols, rows).astype(bf16)
        x_ref[:, cols] = value
        scale = dot(weight, spread[:, cols], ((0,), (0,)))
        scaled = (value.astype(f32) * scale).astype(bf16)
        payload_ref[:, cols] = dot(keys, scaled, ((0,), (0,))).astype(bf16)
    heads = raw_ref.shape[0]
    total = jnp.exp(dot(jnp.ones((half, rows), f32), decay, ((1,), (1,)), highest))
    high = total.astype(bf16)
    payload_ref[:, width:] = jnp.zeros((half, LANES), bf16)
    payload_ref[:, width : width + heads] = high
    payload_ref[:, width + SPREAD : width + SPREAD + heads] = (total - high.astype(f32)).astype(bf16)


def inside_kernel(x_ref, bc_ref, raw_ref, step_bias_ref, decay_ref, skip_ref, y_ref):
    rows = x_ref.shape[0]
    half = bc_ref.shape[1] // 2
    heads = raw_ref.shape[0]
    size, decay = steps(raw_ref, step_bias_ref, decay_ref)
    tri = lower(rows)
    cum = dot(decay, tri, ((1,), (1,)), highest) * LOG2E
    col = dot(tri, decay, ((1,), (1,)), highest) * LOG2E
    row = cum - jnp.log(size) * LOG2E
    mid = rows // 2
    scores = dot(bc_ref[:, half:], bc_ref[:, :half], ((1,), (1,)))
    causal = tri[:mid, :mid] > 0.5
    top = jnp.where(causal, scores[:mid, :mid], 0.0)
    low_left = scores[mid:, :mid]
    low_right = jnp.where(causal, scores[mid:, mid:], 0.0)
    for h in range(heads):
        cols = slice(h * HEAD_DIM, (h + 1) * HEAD_DIM)
        x = x_ref[:, cols]
        c0, c1 = col[:mid, h : h + 1], col[mid:, h : h + 1]
        r0, r1 = row[h : h + 1, :mid], row[h : h + 1, mid:]
        w0 = (top * jnp.exp2(jnp.minimum(c0 - r0, 100.0))).astype(bf16)
        w1 = (low_left * jnp.exp2(c1 - r0)).astype(bf16)
        w2 = (low_right * jnp.exp2(jnp.minimum(c1 - r1, 100.0))).astype(bf16)
        gain = skip_ref[h, 0]
        y_ref[:mid, cols] = dot(w0, x[:mid], ((1,), (0,))) + gain * x[:mid].astype(f32)
        y_ref[mid:, cols] = (
            dot(w1, x[:mid], ((1,), (0,))) + dot(w2, x[mid:], ((1,), (0,)))
            + gain * x[mid:].astype(f32)
        )


def prefix_kernel(devices, got_ref, out_ref):
    width = out_ref.shape[1]
    each = got_ref.shape[0] // devices
    spread = spread_matrix(width)
    decays = dot(got_ref[:, width:], spread, ((1,), (0,)))
    update = got_ref[:, :width].astype(f32)
    running = jnp.zeros((each, width), f32)
    found = []
    for d in range(devices):
        found.append(running)
        rows = slice(d * each, (d + 1) * each)
        if d < devices - 1:
            running = running * decays[rows] + update[rows]
    out_ref[...] = jnp.concatenate(found, axis=0).astype(bf16)


def gate_kernel(
    me_ref, entering_ref, bc_ref, y_ref, raw_ref, step_bias_ref, decay_ref,
    gate_ref, gain_ref, weight_ref, gated_ref, squares_ref, send_ref, parts,
):
    rows, width = y_ref.shape
    half = bc_ref.shape[1] // 2
    _, decay = steps(raw_ref, step_bias_ref, decay_ref)
    cum = jnp.exp(dot(decay, lower(rows), ((1,), (1,)), highest))
    factor = split_rows(parts, cum)
    spread = spread_matrix(width)
    query = bc_ref[:, half:]
    squares = jnp.zeros((rows, LANES), f32)
    block = 256
    for start in range(0, width, block):
        cols = slice(start, start + block)
        carried = dot(query, entering_ref[:, cols], ((1,), (0,)))
        scale = dot(factor, spread[:, cols], ((0,), (0,)))
        mixed = y_ref[:, cols] + carried * scale
        raw = mixed * silu(gate_ref[:, cols].astype(f32))
        for lane in range(0, block, LANES):
            piece = raw[:, lane : lane + LANES]
            squares = squares + piece * piece
        gated_ref[:, cols] = (raw * gain_ref[:, cols]).astype(bf16)
    total = jnp.sum(squares, axis=1, keepdims=True)
    squares_ref[...] = jnp.broadcast_to(total, (rows, LANES))
    high = total.astype(bf16)
    low = (total - high.astype(f32)).astype(bf16)
    lane = lax.broadcasted_iota(jnp.int32, (rows, LANES), 1)
    send_ref[:, width:] = jnp.where(
        lane < SPREAD,
        jnp.broadcast_to(high.astype(f32), (rows, LANES)),
        jnp.broadcast_to(low.astype(f32), (rows, LANES)),
    ).astype(bf16)
    peer = pl.multiple_of((1 - me_ref[0, 0]) * width, LANES)
    send_ref[:, :width] = dot(
        gated_ref[...], weight_ref[:, pl.ds(peer, width)], ((1,), (0,))
    ).astype(bf16)


def own_kernel(me_ref, gated_ref, weight_ref, own_ref):
    width = gated_ref.shape[1]
    mine = pl.multiple_of(me_ref[0, 0] * width, LANES)
    own_ref[...] = dot(gated_ref[...], weight_ref[:, pl.ds(mine, width)], ((1,), (0,)))


def finish_kernel(inner, own_ref, squares_ref, got_ref, out_ref):
    width = own_ref.shape[1]
    other = got_ref[:, width:].astype(f32)
    total = squares_ref[:, :1] + other[:, :1] + other[:, SPREAD : SPREAD + 1]
    scale = lax.rsqrt(total / inner + 1e-05)
    out_ref[...] = ((own_ref[...] + got_ref[:, :width].astype(f32)) * scale).astype(bf16)


VMEM = pl.BlockSpec(memory_space=pltpu.VMEM)
SMEM = pl.BlockSpec(memory_space=pltpu.SMEM)


def call(kernel, specs, outs, flops, scratch=(), limit=40):
    one = not isinstance(outs, (list, tuple))
    return pl.pallas_call(
        kernel,
        out_shape=outs,
        in_specs=specs,
        out_specs=VMEM if one else [VMEM] * len(outs),
        scratch_shapes=list(scratch),
        compiler_params=pltpu.CompilerParams(vmem_limit_bytes=limit << 20),
        cost_estimate=pl.CostEstimate(flops=int(flops), bytes_accessed=1 << 20, transcendentals=0),
    )


def local(
    inner_input, gate_input, state_input, step_raw, conv_inner, conv_state,
    bias_inner, bias_state, step_bias, decay_log, skip_gain, norm_gain, out_weight,
):
    rows, width = inner_input.shape
    heads = step_raw.shape[0]
    states = state_input.shape[1]
    half = states // 2
    devices = lax.axis_size("seq")
    halo = lax.ppermute(
        jnp.concatenate([inner_input[rows - 8 :], state_input[rows - 8 :]], axis=1),
        "seq",
        [(d, d + 1) for d in range(devices - 1)],
    )
    step_args = (step_raw, step_bias[:, None], decay_log[:, None])
    shape = jax.ShapeDtypeStruct
    x, bc, payload = call(
        update_kernel,
        [VMEM] * 10,
        [shape((rows, width), bf16), shape((rows, states), bf16), shape((half, width + LANES), bf16)],
        2e9,
        [
            pltpu.VMEM((rows + 8, width), f32),
            pltpu.VMEM((rows + 8, states), f32),
            pltpu.VMEM((2 * SPREAD, rows), f32),
        ],
    )(
        inner_input, state_input, halo, *step_args,
        conv_inner, bias_inner[None], conv_state, bias_state[None],
    )
    each = half // devices
    got = lax.all_to_all(
        payload.reshape(devices, each, width + LANES), "seq", split_axis=0, concat_axis=0, tiled=True
    )
    y = call(inside_kernel, [VMEM] * 5 + [SMEM], shape((rows, width), f32), 4e9)(
        x, bc, *step_args, skip_gain[:, None]
    )
    before = call(
        functools.partial(prefix_kernel, devices), [VMEM], shape((half, width), bf16), 1e8
    )(got.reshape(half, width + LANES))
    entering = lax.all_to_all(
        before.reshape(devices, each, width), "seq", split_axis=0, concat_axis=0, tiled=True
    ).reshape(half, width)
    me = lax.axis_index("tp").astype(jnp.int32).reshape(1, 1)
    gated, squares, send = call(
        gate_kernel,
        [SMEM] + [VMEM] * 9,
        [shape((rows, width), bf16), shape((rows, LANES), f32), shape((rows, width + LANES), bf16)],
        2e9,
        [pltpu.VMEM((2 * SPREAD, rows), f32)],
    )(me, entering, bc, y, *step_args, gate_input, norm_gain[None], out_weight)
    pairs = lax.axis_size("tp")
    other = lax.ppermute(send, "tp", [(d, pairs - 1 - d) for d in range(pairs)])
    own = call(own_kernel, [SMEM, VMEM, VMEM], shape((rows, width), f32), 2e9)(
        me, gated, out_weight
    )
    return call(
        functools.partial(finish_kernel, float(width * pairs)),
        [VMEM] * 3, shape((rows, width), bf16), 1e8,
    )(own, squares, other)


def solution(mesh):
    return jax.shard_map(
        local,
        mesh=mesh,
        in_specs=(
            P("seq", "tp"), P("seq", "tp"), P("seq", None), P("tp", "seq"), P(None, "tp"), P(),
            P("tp"), P(), P("tp"), P("tp"), P("tp"), P("tp"), P("tp", None),
        ),
        out_specs=P("seq", "tp"),
        check_vma=False,
    )
```

time: 132 us -> 59.8 us (0.45)
  blocking collectives: 47.6 us -> 17.7 us
  matrix products: 14.4 us -> 0 us
  between operations: 14.5 us -> 0.11 us
  Pallas kernels: 0 us -> 11.9 us
  waiting for transfers between devices: 16.5 us -> 6.58 us
  starting transfers between devices: 18 us -> 8.5 us
  other arithmetic: 8.9 us -> 0.01 us
  local copies, waits for them, and re-layouts: 11 us -> 14.3 us
    unnamed x1 -> x0, blocking collectives: 45.1 us -> none
    all_to_all x0 -> x1, blocking collectives: none -> 17.7 us  [local(): lax.all_to_all(payload.reshape(devices, each, width + LANES), 'seq', spli...]
    dot_general x4 -> x0, matrix products: 12 us -> none  [the longest x1 6.31 us: local(): partial_out = jnp.dot(gated, out_weight, preferred_element_type=jnp.float32)]
    pallas_call x0 -> x6, Pallas kernels: none -> 11.9 us  [the longest x1 3.66 us: local(): call(inside_kernel, [VMEM] * 5 + [SMEM], shape((rows, width), f32), 40000...]
    unnamed x22 -> x24, local copies, waits for them, and re-layouts: 2.13 us -> 10.5 us
    reduce_scatter x1 -> x0, waiting for transfers between devices: 6.21 us -> none  [local(): lax.psum_scatter(partial_out, 'tp', scatter_dimension=1, tiled=True)]
    all_to_all x2 -> x1, starting transfers between devices: 9.52 us -> 3.56 us  [local(): lax.all_to_all(before.reshape(devices, each, width), 'seq', split_axis=0,...]
    convert_element_type x5 -> x0, other arithmetic: 5.07 us -> none  [the longest x1 2.29 us: local(): return (summed * scale_inv[:, None]).astype(jnp.bfloat16)]
  transfers between devices with their start and end apart: 5 -> 3, of which waited for: 2 -> 1; matrix products, arithmetic and copies ran while one was open for 9% -> 4% of each run, Pallas kernels for 0% -> 8%
where the time goes in v1:
time: 59.8 us; the launch traced here: 59.1 us
  blocking collectives  17.7 us (30%)
  local copies, waits for them, and re-layouts  14.3 us (24%)
  Pallas kernels  11.9 us (20%)
  starting transfers between devices  8.5 us (14%)
  waiting for transfers between devices  6.58 us (11%)
    all_to_all x1, blocking collectives, local(): lax.all_to_all(payload.reshape(devices, each, width + LANES), 'seq', spli...  17.7 us
    unnamed x24, local copies, waits for them, and re-layouts  10.5 us
    all_to_all x1, waiting for transfers between devices, local(): lax.all_to_all(before.reshape(devices, each, width), 'seq', split_axis=0,...  6.58 us
    ppermute x1, starting transfers between devices, local(): lax.ppermute(jnp.concatenate([inner_input[rows - 8:], state_input[rows -...  4.86 us
    pallas_call x1, Pallas kernels, local(): call(inside_kernel, [VMEM] * 5 + [SMEM], shape((rows, width), f32), 40000...  3.66 us
    all_to_all x1, starting transfers between devices, local(): lax.all_to_all(before.reshape(devices, each, width), 'seq', split_axis=0,...  3.56 us
    pallas_call x1, Pallas kernels, local(): call(update_kernel, [VMEM] * 10, [shape((rows, width), bf16), shape((rows...  3.11 us
    pallas_call x1, Pallas kernels, local(): call(gate_kernel, [SMEM] + [VMEM] * 9, [shape((rows, width), bf16), shape...  2.04 us
  transfers between devices with their start and end apart: 3, of which 1 were waited for; matrix products, arithmetic and copies ran while one was open for 4% of the time, Pallas kernels for 8%

profile of v1, /device:TPU:0, one launch (start us, length us, event | category | flops | bytes accessed | tf_op | source)
XLA Modules:
  0.0 59.1 jit_solution(5419763572485980642)
XLA Ops:
  0.0 0.7 %slice.7 = bf16[8,256]{1,0:T(8,128)(2,1)S(1)} slice(bf16[256,256]{1,0:T(8,128)(2,1)} %state_ref.1), slice={[248:256], [0:256]} | slice | bytes 8192 | tf_op jit(solution)/shard_map/slice | solution.py:230
  0.7 0.7 %slice.6 = bf16[8,1280]{1,0:T(8,128)(2,1)S(1)} slice(bf16[256,1280]{1,0:T(8,128)(2,1)} %inner_ref.1), slice={[248:256], [0:1280]} | slice | bytes 40960 | tf_op jit(solution)/shard_map/slice | solution.py:230
  1.4 4.9 %collective-permute-start = (bf16[8,1536]{1,0:T(8,128)(2,1)S(1)}, bf16[8,1536]{1,0:T(8,128)(2,1)S(1)}, u32[]{:S(2)}, u32[]{:S(2)}) collective-permute-start(bf16[8,1536]{1,0:T(8,128)(2,1)S(1)} %pad_maximum_fusion), channel_id=1, source_target_pairs={{0,2},{2,4},{4,6},{6,8},{8,10},{10,12},{12,14},{14,16},{16,18},{18... | collective-permute-start | bytes 73736 | tf_op jit(solution)/shard_map/ppermute | solution.py:229
  6.3 0.7 %broadcast_in_dim.20.bias_ref = f32[1,1280]{1,0:T(1,128)S(1)} reshape(f32[1280]{0:T(1024)} %param.19) | data formatting | bytes 10240 | tf_op jit(solution)/shard_map/broadcast_in_dim | solution.py:248
  7.0 0.7 %copy.14.step_bias_ref = f32[20,1]{1,0:T(8,128)S(1)} copy(f32[20,1]{0,1:T(1,128)} %bitcast.13) | data formatting | bytes 160 | tf_op jit(solution)/shard_map/broadcast_in_dim | solution.py:234
  7.7 0.7 %copy.15.decay_ref = f32[20,1]{1,0:T(8,128)S(1)} copy(f32[20,1]{0,1:T(1,128)} %bitcast.14) | data formatting | bytes 160 | tf_op jit(solution)/shard_map/broadcast_in_dim | solution.py:234
  8.5 0.0 collective-permute-done.halo_ref
  8.5 0.0 copy-start.3
  8.5 0.7 %copy-done.3 = f32[20,256]{1,0:T(8,128)S(1)} copy-done((f32[20,256]{1,0:T(8,128)S(1)}, f32[20,256]{1,0:T(8,128)}, u32[]{:S(2)}) %copy-start.3) | copy-done | bytes 20504
  9.2 0.0 copy-start.5
  9.2 1.1 %copy-done.5 = bf16[256,1280]{1,0:T(8,128)(2,1)S(1)} copy-done((bf16[256,1280]{1,0:T(8,128)(2,1)S(1)}, bf16[256,1280]{1,0:T(8,128)(2,1)}, u32[]{:S(2)}) %copy-start.5) | copy-done | bytes 655384
  10.3 0.0 copy-start.6
  10.3 0.9 %copy-done.6 = bf16[256,256]{1,0:T(8,128)(2,1)S(1)} copy-done((bf16[256,256]{1,0:T(8,128)(2,1)S(1)}, bf16[256,256]{1,0:T(8,128)(2,1)}, u32[]{:S(2)}) %copy-start.6) | copy-done | bytes 131096
  11.2 0.0 copy-start.7
  11.2 0.7 %copy-done.7 = f32[4,1280]{1,0:T(4,128)S(1)} copy-done((f32[4,1280]{1,0:T(4,128)S(1)}, f32[4,1280]{1,0:T(4,128)}, u32[]{:S(2)}) %copy-start.7) | copy-done | bytes 20504
  11.9 0.0 copy-start.8
  12.0 0.7 %copy-done.8 = f32[4,256]{1,0:T(4,128)S(1)} copy-done((f32[4,256]{1,0:T(4,128)S(1)}, f32[4,256]{1,0:T(4,128)}, u32[]{:S(2)}) %copy-start.8) | copy-done | bytes 4120
  12.6 0.0 copy-start.9
  12.6 0.7 %copy-done.9 = f32[256]{0:T(256)S(1)} copy-done((f32[256]{0:T(256)S(1)}, f32[256]{0:T(256)}, u32[]{:S(2)}) %copy-start.9) | copy-done | bytes 1048
  13.3 3.1 %shard_map.127 = (bf16[256,1280]{1,0:T(8,128)(2,1)S(1)}, bf16[256,256]{1,0:T(8,128)(2,1)S(1)}, bf16[128,1408]{1,0:T(8,128)(2,1)S(1)}) custom-call(bf16[256,1280]{1,0:T(8,128)(2,1)S(1)} %copy-done.5, bf16[256,256]{1,0:T(8,128)(2,1)S(1)} %copy-done.6, bf16[8,1536]{1,0:T(8,128)(2,1)S(1)} %collective-permute-done.halo_ref, f32[20,256]{1,0:T(8,128)S(1)} %copy-done.3, ...), custom_call_target="tpu_custom_call" | custom-call | flops 2000000000 | bytes 1048576 | tf_op jit(solution)/shard_map/pallas_call | solution.py:236
  16.4 0.0 copy-start.10
  16.4 0.0 copy-start.11
  16.4 0.0 copy-start.4
  16.4 17.7 %all_to_all.10 = bf16[16,8,1408]{2,1,0:T(8,128)(2,1)S(1)} all-to-all(bf16[16,8,1408]{2,1,0:T(8,128)(2,1)S(1)} %bitcast.11), channel_id=1, replica_groups=mesh['seq'=16,'tp'=2] {'seq'}, dimensions={0} | all-to-all | bytes 720896 | tf_op jit(solution)/shard_map/all_to_all | solution.py:251
  34.2 1.0 %shard_map.128 = bf16[128,1280]{1,0:T(8,128)(2,1)} custom-call(bf16[128,1408]{1,0:T(8,128)(2,1)S(1)} %bitcast.9), custom_call_target="tpu_custom_call" | custom-call | flops 100000000 | bytes 1048576 | tf_op jit(solution)/shard_map/pallas_call | solution.py:257
  35.1 3.6 %all-to-all-start.1 = ((bf16[16,8,1280]{2,1,0:T(8,128)(2,1)}), bf16[16,8,1280]{2,1,0:T(8,128)(2,1)S(1)}, u32[]{:S(2)}, u32[]{:S(2)}) async-start(bf16[16,8,1280]{2,1,0:T(8,128)(2,1)} %bitcast.6), calls=%async_computation.1 | async-start | bytes 655360 | tf_op jit(solution)/shard_map/all_to_all | solution.py:260
  38.7 0.0 copy-done.10
  38.7 0.0 copy-done.11
  38.7 0.1 copy.18.skip_ref
  38.8 0.0 copy-done.4
  38.8 0.0 copy-start.2
  38.8 3.7 %shard_map.129.y_ref = f32[256,1280]{1,0:T(8,128)S(1)} custom-call(bf16[256,1280]{1,0:T(8,128)(2,1)S(1)} %get-tuple-element.13.x_ref, bf16[256,256]{1,0:T(8,128)(2,1)S(1)} %get-tuple-element.12.bc_ref, f32[20,256]{1,0:T(8,128)S(1)} %copy-done.4, f32[20,1]{1,0:T(8,128)S(1)} %copy.14.step_bias_ref, f32[20,1]{1,0:T(8,128)S(1)} %copy.15.decay_ref, ...), custom_call_target="tpu_custom_call" | custom-call | flops 4000000000 | bytes 1048576 | tf_op jit(solution)/shard_map/pallas_call | solution.py:254
  42.5 6.6 %all-to-all-done.1 = bf16[16,8,1280]{2,1,0:T(8,128)(2,1)S(1)} async-done(((bf16[16,8,1280]{2,1,0:T(8,128)(2,1)}), bf16[16,8,1280]{2,1,0:T(8,128)(2,1)S(1)}, u32[]{:S(2)}, u32[]{:S(2)}) %all-to-all-start.1) | async-done | bytes 327712 | tf_op jit(solution)/shard_map/all_to_all | solution.py:260
  49.1 0.0 copy-done.2
  49.1 0.0 copy-start
  49.1 2.9 %copy-done = bf16[1280,2560]{1,0:T(8,128)(2,1)S(1)} copy-done((bf16[1280,2560]{1,0:T(8,128)(2,1)S(1)}, bf16[1280,2560]{1,0:T(8,128)(2,1)}, u32[]{:S(2)}) %copy-start) | copy-done | bytes 6553624
  52.0 2.0 %shard_map.130 = (bf16[256,1280]{1,0:T(8,128)(2,1)S(1)}, f32[256,128]{1,0:T(8,128)S(1)}, bf16[256,1408]{1,0:T(8,128)(2,1)S(1)}) custom-call(s32[1,1]{1,0:T(1,128)} %bitcast.me_ref, bf16[128,1280]{1,0:T(8,128)(2,1)S(1)} %bitcast.10, bf16[256,256]{1,0:T(8,128)(2,1)S(1)} %get-tuple-element.12.bc_ref, f32[256,1280]{1,0:T(8,128)S(1)} %shard_map.129.y_ref, ...), custom_call_target="tpu_custom_call" | custom-call | flops 2000000000 | bytes 1048576 | tf_op jit(solution)/shard_map/pallas_call | solution.py:264
  54.0 0.1 collective-permute-start.1
  54.1 0.0 copy-start.1
  54.1 2.9 %copy-done.1 = bf16[1280,2560]{1,0:T(8,128)(2,1)S(1)} copy-done((bf16[1280,2560]{1,0:T(8,128)(2,1)S(1)}, bf16[1280,2560]{1,0:T(8,128)(2,1)}, u32[]{:S(2)}) %copy-start.1) | copy-done | bytes 6553624
  56.9 1.0 %shard_map.131.own_ref = f32[256,1280]{1,0:T(8,128)S(1)} custom-call(s32[1,1]{1,0:T(1,128)} %bitcast.me_ref, bf16[256,1280]{1,0:T(8,128)(2,1)S(1)} %get-tuple-element.14.gated_ref, bf16[1280,2560]{1,0:T(8,128)(2,1)S(1)} %copy-done.1), custom_call_target="tpu_custom_call" | custom-call | flops 2000000000 | bytes 1048576 | tf_op jit(solution)/shard_map/pallas_call | solution.py:273
  58.0 0.0 collective-permute-done.1.got_ref
  58.0 1.1 %shard_map.132 = bf16[256,1280]{1,0:T(8,128)(2,1)} custom-call(f32[256,1280]{1,0:T(8,128)S(1)} %shard_map.131.own_ref, f32[256,128]{1,0:T(8,128)S(1)} %get-tuple-element.15.squares_ref, bf16[256,1408]{1,0:T(8,128)(2,1)S(1)} %collective-permute-done.1.got_ref), custom_call_target="tpu_custom_call" | custom-call | flops 100000000 | bytes 1048576 | tf_op jit(solution)/shard_map/pallas_call | solution.py:276
  (2 shorter events, 0.0 us)
Async XLA Ops:
  1.4 7.1 %collective-permute-start = (bf16[8,1536]{1,0:T(8,128)(2,1)S(1)}, bf16[8,1536]{1,0:T(8,128)(2,1)S(1)}, u32[]{:S(2)}, u32[]{:S(2)}) collective-permute-start(bf16[8,1536]{1,0:T(8,128)(2,1)S(1)} %pad_maximum_fusion), channel_id=1, source_target_pairs={{0,2},{2,4},{4,6},{6,8},{8,10},{10,12},{12,14},{14,16},{16,18},{18... | collective-permute-start | bytes 73736 | tf_op jit(solution)/shard_map/ppermute | solution.py:229
  8.5 0.7 %copy-start.3 = (f32[20,256]{1,0:T(8,128)S(1)}, f32[20,256]{1,0:T(8,128)}, u32[]{:S(2)}) copy-start(f32[20,256]{1,0:T(8,128)} %raw_ref.5) | copy-start | bytes 61444
  9.2 1.1 %copy-start.5 = (bf16[256,1280]{1,0:T(8,128)(2,1)S(1)}, bf16[256,1280]{1,0:T(8,128)(2,1)}, u32[]{:S(2)}) copy-start(bf16[256,1280]{1,0:T(8,128)(2,1)} %inner_ref.1) | copy-start | bytes 1966084
  10.3 0.9 %copy-start.6 = (bf16[256,256]{1,0:T(8,128)(2,1)S(1)}, bf16[256,256]{1,0:T(8,128)(2,1)}, u32[]{:S(2)}) copy-start(bf16[256,256]{1,0:T(8,128)(2,1)} %state_ref.1) | copy-start | bytes 393220
  11.2 0.7 %copy-start.7 = (f32[4,1280]{1,0:T(4,128)S(1)}, f32[4,1280]{1,0:T(4,128)}, u32[]{:S(2)}) copy-start(f32[4,1280]{1,0:T(4,128)} %taps_ref.1) | copy-start | bytes 61444
  11.9 0.7 %copy-start.8 = (f32[4,256]{1,0:T(4,128)S(1)}, f32[4,256]{1,0:T(4,128)}, u32[]{:S(2)}) copy-start(f32[4,256]{1,0:T(4,128)} %state_taps_ref.1) | copy-start | bytes 12292
  12.6 0.7 %copy-start.9 = (f32[256]{0:T(256)S(1)}, f32[256]{0:T(256)}, u32[]{:S(2)}) copy-start(f32[256]{0:T(256)} %param.20) | copy-start | bytes 3076
  16.4 22.3 %copy-start.10 = (f32[1280]{0:T(1024)S(1)}, f32[1280]{0:T(1024)}, u32[]{:S(2)}) copy-start(f32[1280]{0:T(1024)} %param.24) | copy-start | bytes 15364
  16.4 22.3 %copy-start.11 = (f32[20]{0:T(128)S(1)}, f32[20]{0:T(128)}, u32[]{:S(2)}) copy-start(f32[20]{0:T(128)} %param.23) | copy-start | bytes 244
  16.4 22.4 %copy-start.4 = (f32[20,256]{1,0:T(8,128)S(1)}, f32[20,256]{1,0:T(8,128)}, u32[]{:S(2)}) copy-start(f32[20,256]{1,0:T(8,128)} %raw_ref.5) | copy-start | bytes 61444
  35.1 14.0 %all-to-all-start.1 = ((bf16[16,8,1280]{2,1,0:T(8,128)(2,1)}), bf16[16,8,1280]{2,1,0:T(8,128)(2,1)S(1)}, u32[]{:S(2)}, u32[]{:S(2)}) async-start(bf16[16,8,1280]{2,1,0:T(8,128)(2,1)} %bitcast.6), calls=%async_computation.1 | async-start | bytes 655360 | tf_op jit(solution)/shard_map/all_to_all | solution.py:260
  38.8 10.3 %copy-start.2 = (bf16[256,1280]{1,0:T(8,128)(2,1)S(1)}, bf16[256,1280]{1,0:T(8,128)(2,1)}, u32[]{:S(2)}) copy-start(bf16[256,1280]{1,0:T(8,128)(2,1)} %gate_ref.1) | copy-start | bytes 1966084
  49.1 2.9 %copy-start = (bf16[1280,2560]{1,0:T(8,128)(2,1)S(1)}, bf16[1280,2560]{1,0:T(8,128)(2,1)}, u32[]{:S(2)}) copy-start(bf16[1280,2560]{1,0:T(8,128)(2,1)} %weight_ref.3) | copy-start | bytes 19660804
  54.0 4.0 %collective-permute-start.1 = (bf16[256,1408]{1,0:T(8,128)(2,1)S(1)}, bf16[256,1408]{1,0:T(8,128)(2,1)S(1)}, u32[]{:S(2)}, u32[]{:S(2)}) collective-permute-start(bf16[256,1408]{1,0:T(8,128)(2,1)S(1)} %get-tuple-element.16), channel_id=1, source_target_pairs={{0,1},{1,0},{2,3},{3,2},{4,5},{5,4},{6,7},{7,6},{8,9},{9,8},{10,11... | collective-permute-start | bytes 2162696 | tf_op jit(solution)/shard_map/ppermute | solution.py:272
  54.1 2.9 %copy-start.1 = (bf16[1280,2560]{1,0:T(8,128)(2,1)S(1)}, bf16[1280,2560]{1,0:T(8,128)(2,1)}, u32[]{:S(2)}) copy-start(bf16[1280,2560]{1,0:T(8,128)(2,1)} %weight_ref.3) | copy-start | bytes 19660804

commit v2 on v1

--- a/solution.py
+++ b/solution.py
@@ -37,15 +37,22 @@
     ref[...] = jnp.zeros_like(ref)
     ref[0:heads, :] = high
     ref[SPREAD : SPREAD + heads, :] = value - high
-    return ref[...].astype(bf16)
+    return ref[...].T.astype(bf16)
+
+
+def as_column(row):
+    count = row.shape[1]
+    a = lax.broadcasted_iota(jnp.int32, (count, count), 0)
+    b = lax.broadcasted_iota(jnp.int32, (count, count), 1)
+    return jnp.sum(jnp.where(a == b, jnp.broadcast_to(row, (count, count)), 0.0), axis=1, keepdims=True)
 
 
 def steps(raw_ref, step_bias_ref, decay_ref):
-    v = raw_ref[...] + step_bias_ref[...]
+    v = raw_ref[...] + as_column(step_bias_ref[...])
     x = jnp.exp(-jnp.abs(v))
     series = x * (1.0 - x * (0.5 - x * (1.0 / 3.0 - x * 0.25)))
     size = jnp.maximum(v, 0.0) + jnp.where(x < 0.01, series, jnp.log(1.0 + x))
-    return size, -jnp.exp(decay_ref[...]) * size
+    return size, -jnp.exp(as_column(decay_ref[...])) * size
 
 
 def lower(rows):
@@ -54,10 +61,15 @@
     return jnp.where(t >= s, 1.0, 0.0).astype(f32)
 
 
+def row_of(ref, cols):
+    first, last = cols.start // LANES, cols.stop // LANES
+    return jnp.concatenate([ref[r : r + 1, :] for r in range(first, last)], axis=1)
+
+
 def conv_block(scratch, taps_ref, bias_ref, cols, rows):
     taps = taps_ref.shape[0]
     first = 8 - (taps - 1)
-    total = jnp.broadcast_to(bias_ref[:, cols], (rows, bias_ref[:, cols].shape[1]))
+    total = jnp.broadcast_to(row_of(bias_ref, cols), (rows, cols.stop - cols.start))
     for number in range(taps):
         total = total + taps_ref[number : number + 1, cols] * scratch[
             pl.ds(first + number, rows), cols
@@ -65,39 +77,66 @@
     return silu(total)
 
 
-def update_kernel(
-    inner_ref, state_ref, halo_ref, raw_ref, step_bias_ref, decay_ref,
-    taps_ref, bias_ref, state_taps_ref, state_bias_ref,
-    x_ref, bc_ref, payload_ref, pad, state_pad, parts,
-):
+def update_kernel(count, *refs):
+    sources, (x_out, bc_out, payload_out) = refs[:count], refs[count : count + 3]
+    kept, rest = refs[count + 3 : 2 * count + 3], refs[2 * count + 3 :]
+    (
+        halo_ref, raw_ref, step_bias_ref, decay_ref, state_taps_ref, state_bias_ref, state_ref,
+        taps_ref, bias_ref, inner_ref,
+    ) = kept
+    x_ref, bc_ref, payload_ref, pad, state_pad, parts, in_sems, out_sems = rest
+    copies = [
+        pltpu.make_async_copy(a, b, in_sems.at[i]) for i, (a, b) in enumerate(zip(sources, kept))
+    ]
+    for copy in copies:
+        copy.start()
+    for copy in copies[:-1]:
+        copy.wait()
     rows, width = inner_ref.shape
+    leaving = []
+
+    def leave(source, target):
+        copy = pltpu.make_async_copy(source, target, out_sems.at[len(leaving)])
+        copy.start()
+        leaving.append(copy)
+
     states = state_ref.shape[1]
     half = states // 2
     state_pad[0:8, :] = halo_ref[:, width:].astype(f32)
     state_pad[8:, :] = state_ref[...].astype(f32)
     bc_ref[...] = conv_block(state_pad, state_taps_ref, state_bias_ref, slice(0, states), rows).astype(bf16)
-    keys = bc_ref[:, :half]
+    leave(bc_ref, bc_out)
+    keys = bc_ref[:, :half].astype(f32).T.astype(bf16)
     size, decay = steps(raw_ref, step_bias_ref, decay_ref)
+    heads = raw_ref.shape[0]
+    parts[...] = jnp.zeros_like(parts)
+    parts[0:heads, :] = decay
+    parts[SPREAD : SPREAD + heads, :] = decay
+    total = jnp.exp(dot(jnp.ones((half, rows), f32), parts[...], ((1,), (1,)), highest))
+    high = total.astype(bf16).astype(f32)
+    lane = lax.broadcasted_iota(jnp.int32, (half, LANES), 1)
+    payload_ref[:, width:] = jnp.where(lane < SPREAD, high, total - high).astype(bf16)
     cum = dot(decay, lower(rows), ((1,), (1,)), highest)
     weight = jnp.exp(cum[:, rows - 1 :] - cum) * size
     weight = split_rows(parts, weight)
     spread = spread_matrix(width)
+    copies[-1].wait()
     pad[0:8, :] = halo_ref[:, :width].astype(f32)
     pad[8:, :] = inner_ref[...].astype(f32)
+    last = slice(width, width + LANES)
+    leave(payload_ref.at[:, last], payload_out.at[:, last])
     block = 256
     for start in range(0, width, block):
         cols = slice(start, start + block)
         value = conv_block(pad, taps_ref, bias_ref, cols, rows).astype(bf16)
         x_ref[:, cols] = value
-        scale = dot(weight, spread[:, cols], ((0,), (0,)))
+        leave(x_ref.at[:, cols], x_out.at[:, cols])
+        scale = dot(weight, spread[:, cols], ((1,), (0,)))
         scaled = (value.astype(f32) * scale).astype(bf16)
-        payload_ref[:, cols] = dot(keys, scaled, ((0,), (0,))).astype(bf16)
-    heads = raw_ref.shape[0]
-    total = jnp.exp(dot(jnp.ones((half, rows), f32), decay, ((1,), (1,)), highest))
-    high = total.astype(bf16)
-    payload_ref[:, width:] = jnp.zeros((half, LANES), bf16)
-    payload_ref[:, width : width + heads] = high
-    payload_ref[:, width + SPREAD : width + SPREAD + heads] = (total - high.astype(f32)).astype(bf16)
+        payload_ref[:, cols] = dot(keys, scaled, ((1,), (0,))).astype(bf16)
+        leave(payload_ref.at[:, cols], payload_out.at[:, cols])
+    for copy in leaving:
+        copy.wait()
 
 
 def inside_kernel(x_ref, bc_ref, raw_ref, step_bias_ref, decay_ref, skip_ref, y_ref):
@@ -123,7 +162,7 @@
         w0 = (top * jnp.exp2(jnp.minimum(c0 - r0, 100.0))).astype(bf16)
         w1 = (low_left * jnp.exp2(c1 - r0)).astype(bf16)
         w2 = (low_right * jnp.exp2(jnp.minimum(c1 - r1, 100.0))).astype(bf16)
-        gain = skip_ref[h, 0]
+        gain = skip_ref[h]
         y_ref[:mid, cols] = dot(w0, x[:mid], ((1,), (0,))) + gain * x[:mid].astype(f32)
         y_ref[mid:, cols] = (
             dot(w1, x[:mid], ((1,), (0,))) + dot(w2, x[mid:], ((1,), (0,)))
@@ -149,9 +188,17 @@
 
 def gate_kernel(
     me_ref, entering_ref, bc_ref, y_ref, raw_ref, step_bias_ref, decay_ref,
-    gate_ref, gain_ref, weight_ref, gated_ref, squares_ref, send_ref, parts,
+    gate_ref, gain_ref, weight_ref, gated_ref, squares_ref, send_ref, mine_ref,
+    parts, theirs_ref, sems,
 ):
     rows, width = y_ref.shape
+    me = me_ref[0, 0]
+    peer = pl.multiple_of((1 - me) * width, LANES)
+    mine = pl.multiple_of(me * width, LANES)
+    first = pltpu.make_async_copy(weight_ref.at[:, pl.ds(peer, width)], theirs_ref, sems.at[0])
+    second = pltpu.make_async_copy(weight_ref.at[:, pl.ds(mine, width)], mine_ref, sems.at[1])
+    first.start()
+    second.start()
     half = bc_ref.shape[1] // 2
     _, decay = steps(raw_ref, step_bias_ref, decay_ref)
     cum = jnp.exp(dot(decay, lower(rows), ((1,), (1,)), highest))
@@ -163,13 +210,13 @@
     for start in range(0, width, block):
         cols = slice(start, start + block)
         carried = dot(query, entering_ref[:, cols], ((1,), (0,)))
-        scale = dot(factor, spread[:, cols], ((0,), (0,)))
+        scale = dot(factor, spread[:, cols], ((1,), (0,)))
         mixed = y_ref[:, cols] + carried * scale
         raw = mixed * silu(gate_ref[:, cols].astype(f32))
         for lane in range(0, block, LANES):
             piece = raw[:, lane : lane + LANES]
             squares = squares + piece * piece
-        gated_ref[:, cols] = (raw * gain_ref[:, cols]).astype(bf16)
+        gated_ref[:, cols] = (raw * row_of(gain_ref, cols)).astype(bf16)
     total = jnp.sum(squares, axis=1, keepdims=True)
     squares_ref[...] = jnp.broadcast_to(total, (rows, LANES))
     high = total.astype(bf16)
@@ -180,16 +227,13 @@
         jnp.broadcast_to(high.astype(f32), (rows, LANES)),
         jnp.broadcast_to(low.astype(f32), (rows, LANES)),
     ).astype(bf16)
-    peer = pl.multiple_of((1 - me_ref[0, 0]) * width, LANES)
-    send_ref[:, :width] = dot(
-        gated_ref[...], weight_ref[:, pl.ds(peer, width)], ((1,), (0,))
-    ).astype(bf16)
-
-
-def own_kernel(me_ref, gated_ref, weight_ref, own_ref):
-    width = gated_ref.shape[1]
-    mine = pl.multiple_of(me_ref[0, 0] * width, LANES)
-    own_ref[...] = dot(gated_ref[...], weight_ref[:, pl.ds(mine, width)], ((1,), (0,)))
+    first.wait()
+    send_ref[:, :width] = dot(gated_ref[...], theirs_ref[...], ((1,), (0,))).astype(bf16)
+    second.wait()
+
+
+def own_kernel(gated_ref, weight_ref, own_ref):
+    own_ref[...] = dot(gated_ref[...], weight_ref[...], ((1,), (0,)))
 
 
 def finish_kernel(inner, own_ref, squares_ref, got_ref, out_ref):
@@ -202,19 +246,24 @@
 
 VMEM = pl.BlockSpec(memory_space=pltpu.VMEM)
 SMEM = pl.BlockSpec(memory_space=pltpu.SMEM)
-
-
-def call(kernel, specs, outs, flops, scratch=(), limit=40):
+HBM = pl.BlockSpec(memory_space=pltpu.HBM)
+
+
+def call(kernel, specs, outs, flops, scratch=(), limit=40 << 20, out=VMEM):
     one = not isinstance(outs, (list, tuple))
     return pl.pallas_call(
         kernel,
         out_shape=outs,
         in_specs=specs,
-        out_specs=VMEM if one else [VMEM] * len(outs),
+        out_specs=out if one else [out] * len(outs),
         scratch_shapes=list(scratch),
-        compiler_params=pltpu.CompilerParams(vmem_limit_bytes=limit << 20),
+        compiler_params=pltpu.CompilerParams(vmem_limit_bytes=limit),
         cost_estimate=pl.CostEstimate(flops=int(flops), bytes_accessed=1 << 20, transcendentals=0),
     )
+
+
+WHOLE = 67043328
+GATE_LIMIT = 44 << 20
 
 
 def local(
@@ -222,7 +271,6 @@
     bias_inner, bias_state, step_bias, decay_log, skip_gain, norm_gain, out_weight,
 ):
     rows, width = inner_input.shape
-    heads = step_raw.shape[0]
     states = state_input.shape[1]
     half = states // 2
     devices = lax.axis_size("seq")
@@ -231,28 +279,36 @@
         "seq",
         [(d, d + 1) for d in range(devices - 1)],
     )
-    step_args = (step_raw, step_bias[:, None], decay_log[:, None])
+    step_args = (step_raw, step_bias[None], decay_log[None])
+    given = (
+        halo, *step_args, conv_state, bias_state.reshape(-1, LANES), state_input,
+        conv_inner, bias_inner.reshape(-1, LANES), inner_input,
+    )
     shape = jax.ShapeDtypeStruct
+    made = [((rows, width), bf16), ((rows, states), bf16), ((half, width + LANES), bf16)]
     x, bc, payload = call(
-        update_kernel,
-        [VMEM] * 10,
-        [shape((rows, width), bf16), shape((rows, states), bf16), shape((half, width + LANES), bf16)],
+        functools.partial(update_kernel, len(given)),
+        [HBM] * len(given),
+        [shape(*m) for m in made],
         2e9,
-        [
+        [pltpu.VMEM(v.shape, v.dtype) for v in given]
+        + [pltpu.VMEM(*m) for m in made]
+        + [
             pltpu.VMEM((rows + 8, width), f32),
             pltpu.VMEM((rows + 8, states), f32),
             pltpu.VMEM((2 * SPREAD, rows), f32),
+            pltpu.SemaphoreType.DMA((len(given),)),
+            pltpu.SemaphoreType.DMA((2 * (width // 256) + 2,)),
         ],
-    )(
-        inner_input, state_input, halo, *step_args,
-        conv_inner, bias_inner[None], conv_state, bias_state[None],
-    )
+        WHOLE,
+        HBM,
+    )(*given)
     each = half // devices
     got = lax.all_to_all(
         payload.reshape(devices, each, width + LANES), "seq", split_axis=0, concat_axis=0, tiled=True
     )
     y = call(inside_kernel, [VMEM] * 5 + [SMEM], shape((rows, width), f32), 4e9)(
-        x, bc, *step_args, skip_gain[:, None]
+        x, bc, *step_args, skip_gain
     )
     before = call(
         functools.partial(prefix_kernel, devices), [VMEM], shape((half, width), bf16), 1e8
@@ -261,18 +317,24 @@
         before.reshape(devices, each, width), "seq", split_axis=0, concat_axis=0, tiled=True
     ).reshape(half, width)
     me = lax.axis_index("tp").astype(jnp.int32).reshape(1, 1)
-    gated, squares, send = call(
+    gated, squares, send, mine = call(
         gate_kernel,
-        [SMEM] + [VMEM] * 9,
-        [shape((rows, width), bf16), shape((rows, LANES), f32), shape((rows, width + LANES), bf16)],
+        [SMEM] + [VMEM] * 8 + [HBM],
+        [
+            shape((rows, width), bf16), shape((rows, LANES), f32),
+            shape((rows, width + LANES), bf16), shape((width, width), bf16),
+        ],
         2e9,
-        [pltpu.VMEM((2 * SPREAD, rows), f32)],
-    )(me, entering, bc, y, *step_args, gate_input, norm_gain[None], out_weight)
+        [
+            pltpu.VMEM((2 * SPREAD, rows), f32),
+            pltpu.VMEM((width, width), bf16),
+            pltpu.SemaphoreType.DMA((2,)),
+        ],
+        GATE_LIMIT,
+    )(me, entering, bc, y, *step_args, gate_input, norm_gain.reshape(-1, LANES), out_weight)
     pairs = lax.axis_size("tp")
     other = lax.ppermute(send, "tp", [(d, pairs - 1 - d) for d in range(pairs)])
-    own = call(own_kernel, [SMEM, VMEM, VMEM], shape((rows, width), f32), 2e9)(
-        me, gated, out_weight
-    )
+    own = call(own_kernel, [VMEM, VMEM], shape((rows, width), f32), 2e9)(gated, mine)
     return call(
         functools.partial(finish_kernel, float(width * pairs)),
         [VMEM] * 3, shape((rows, width), bf16), 1e8,

time: 59.8 us -> 55 us (0.920)
  local copies, waits for them, and re-layouts: 14.3 us -> 6.73 us
  Pallas kernels: 11.9 us -> 15.7 us
  waiting for transfers between devices: 6.58 us -> 4.89 us
  blocking collectives: 17.7 us -> 18.5 us
    unnamed x24 -> x26, local copies, waits for them, and re-layouts: 10.5 us -> 5.31 us
    all_to_all x1, waiting for transfers between devices: 6.58 us -> 2.23 us  [local(): lax.all_to_all(before.reshape(devices, each, width), 'seq', split_axis=0,...]
    pallas_call x3, Pallas kernels: 6.16 us -> 10.2 us  [the longest x1 4.83 us: local(): call(functools.partial(update_kernel, len(given)), [HBM] * len(given), [s...]
    broadcast_in_dim x5 -> x0, local copies, waits for them, and re-layouts: 2.3 us -> none  [the longest x2 1.49 us: local(): step_args = (step_raw, step_bias[:, None], decay_log[:, None])]
    ppermute x1, waiting for transfers between devices: 0.01 us -> 1.5 us  [local(): lax.ppermute(jnp.concatenate([inner_input[rows - 8:], state_input[rows -...]
    ppermute x1, waiting for transfers between devices: 0.01 us -> 1.16 us  [local(): other = lax.ppermute(send, 'tp', [(d, pairs - 1 - d) for d in range(pairs)])]
    all_to_all x1, blocking collectives: 17.7 us -> 18.5 us  [local(): lax.all_to_all(payload.reshape(devices, each, width + LANES), 'seq', spli...]
  transfers between devices with their start and end apart: 3 -> 3, of which waited for: 1 -> 3; matrix products, arithmetic and copies ran while one was open for 4% -> 0% of each run, Pallas kernels for 8% -> 8%
where the time goes in v2:
time: 55 us; the launch traced here: 54.4 us
  blocking collectives  18.5 us (34%)
  Pallas kernels  15.7 us (29%)
  starting transfers between devices  8.5 us (15%)
  local copies, waits for them, and re-layouts  6.73 us (12%)
  waiting for transfers between devices  4.89 us (9%)
    all_to_all x1, blocking collectives, local(): lax.all_to_all(payload.reshape(devices, each, width + LANES), 'seq', spli...  18.5 us
    unnamed x26, local copies, waits for them, and re-layouts  5.31 us
    ppermute x1, starting transfers between devices, local(): lax.ppermute(jnp.concatenate([inner_input[rows - 8:], state_input[rows -...  4.86 us
    pallas_call x1, Pallas kernels, local(): call(functools.partial(update_kernel, len(given)), [HBM] * len(given), [s...  4.83 us
    pallas_call x1, Pallas kernels, local(): call(gate_kernel, [SMEM] + [VMEM] * 8 + [HBM], [shape((rows, width), bf16...  4.35 us
    all_to_all x1, starting transfers between devices, local(): lax.all_to_all(before.reshape(devices, each, width), 'seq', split_axis=0,...  3.56 us
    pallas_call x1, Pallas kernels, local(): call(inside_kernel, [VMEM] * 5 + [SMEM], shape((rows, width), f32), 40000...  3.42 us
    all_to_all x1, waiting for transfers between devices, local(): lax.all_to_all(before.reshape(devices, each, width), 'seq', split_axis=0,...  2.23 us
  transfers between devices with their start and end apart: 3, of which 3 were waited for; matrix products, arithmetic and copies ran while one was open for 0% of the time, Pallas kernels for 8%

profile of v2, /device:TPU:0, one launch (start us, length us, event | category | flops | bytes accessed | tf_op | source)
XLA Modules:
  0.0 54.4 jit_solution(15757156989068528442)
XLA Ops:
  0.0 0.7 %slice.7 = bf16[8,256]{1,0:T(8,128)(2,1)S(1)} slice(bf16[256,256]{1,0:T(8,128)(2,1)} %refs_6_.1), slice={[248:256], [0:256]} | slice | bytes 8192 | tf_op jit(solution)/shard_map/slice | solution.py:278
  0.7 0.7 %slice.6 = bf16[8,1280]{1,0:T(8,128)(2,1)S(1)} slice(bf16[256,1280]{1,0:T(8,128)(2,1)} %refs_9_.1), slice={[248:256], [0:1280]} | slice | bytes 40960 | tf_op jit(solution)/shard_map/slice | solution.py:278
  1.4 4.9 %collective-permute-start = (bf16[8,1536]{1,0:T(8,128)(2,1)S(1)}, bf16[8,1536]{1,0:T(8,128)(2,1)S(1)}, u32[]{:S(2)}, u32[]{:S(2)}) collective-permute-start(bf16[8,1536]{1,0:T(8,128)(2,1)S(1)} %pad_maximum_fusion), channel_id=1, source_target_pairs={{0,2},{2,4},{4,6},{6,8},{8,10},{10,12},{12,14},{14,16},{16,18},{18... | collective-permute-start | bytes 73736 | tf_op jit(solution)/shard_map/ppermute | solution.py:277
  6.3 1.5 %collective-permute-done.refs_0_ = bf16[8,1536]{1,0:T(8,128)(2,1)S(1)} collective-permute-done((bf16[8,1536]{1,0:T(8,128)(2,1)S(1)}, bf16[8,1536]{1,0:T(8,128)(2,1)S(1)}, u32[]{:S(2)}, u32[]{:S(2)}) %collective-permute-start) | collective-permute-done | bytes 24608 | tf_op jit(solution)/shard_map/ppermute | solution.py:277
  7.8 0.0 copy-start.12
  7.8 0.6 %copy-done.12 = bf16[8,1536]{1,0:T(8,128)(2,1)} copy-done((bf16[8,1536]{1,0:T(8,128)(2,1)}, bf16[8,1536]{1,0:T(8,128)(2,1)S(1)}, u32[]{:S(2)}) %copy-start.12) | copy-done | bytes 24600
  8.4 4.8 %shard_map.127 = (bf16[256,1280]{1,0:T(8,128)(2,1)}, bf16[256,256]{1,0:T(8,128)(2,1)}, bf16[128,1408]{1,0:T(8,128)(2,1)}) custom-call(bf16[8,1536]{1,0:T(8,128)(2,1)} %copy-done.12, f32[20,256]{1,0:T(8,128)} %raw_ref.3, f32[1,20]{1,0:T(1,128)} %bitcast.13, f32[1,20]{1,0:T(1,128)} %bitcast.16, f32[4,256]{1,0:T(4,128)} %refs_4_.1, f32[2,128]{1,0:T(2,128)} %bitcast.21, ...), custom_call_target="tpu_custom_call" | custom-call | flops 2000000000 | bytes 1048576 | tf_op jit(solution)/shard_map/pallas_call | solution.py:289
  13.2 18.5 %all_to_all.10 = bf16[16,8,1408]{2,1,0:T(8,128)(2,1)S(1)} all-to-all(bf16[16,8,1408]{2,1,0:T(8,128)(2,1)} %bitcast.19), channel_id=1, replica_groups=mesh['seq'=16,'tp'=2] {'seq'}, dimensions={0} | all-to-all | bytes 720896 | tf_op jit(solution)/shard_map/all_to_all | solution.py:307
  31.7 1.0 %shard_map.128 = bf16[128,1280]{1,0:T(8,128)(2,1)} custom-call(bf16[128,1408]{1,0:T(8,128)(2,1)S(1)} %bitcast.10), custom_call_target="tpu_custom_call" | custom-call | flops 100000000 | bytes 1048576 | tf_op jit(solution)/shard_map/pallas_call | solution.py:313
  32.7 3.6 %all-to-all-start.1 = ((bf16[16,8,1280]{2,1,0:T(8,128)(2,1)}), bf16[16,8,1280]{2,1,0:T(8,128)(2,1)S(1)}, u32[]{:S(2)}, u32[]{:S(2)}) async-start(bf16[16,8,1280]{2,1,0:T(8,128)(2,1)} %bitcast.7), calls=%async_computation.1 | async-start | bytes 655360 | tf_op jit(solution)/shard_map/all_to_all | solution.py:316
  36.3 0.0 copy-start.1
  36.3 0.9 %copy-done.1 = bf16[256,256]{1,0:T(8,128)(2,1)S(1)} copy-done((bf16[256,256]{1,0:T(8,128)(2,1)S(1)}, bf16[256,256]{1,0:T(8,128)(2,1)}, u32[]{:S(2)}) %copy-start.1) | copy-done | bytes 131096
  37.2 0.0 copy-start.3
  37.2 0.7 %copy-done.3 = f32[20,256]{1,0:T(8,128)S(1)} copy-done((f32[20,256]{1,0:T(8,128)S(1)}, f32[20,256]{1,0:T(8,128)}, u32[]{:S(2)}) %copy-start.3) | copy-done | bytes 20504
  37.9 0.0 copy-start.6
  37.9 0.7 %copy-done.6 = f32[20]{0:T(128)S(1)} copy-done((f32[20]{0:T(128)S(1)}, f32[20]{0:T(128)}, u32[]{:S(2)}) %copy-start.6) | copy-done | bytes 104
  38.6 0.0 copy-start.8
  38.6 0.7 %copy-done.8 = f32[20]{0:T(128)S(1)} copy-done((f32[20]{0:T(128)S(1)}, f32[20]{0:T(128)}, u32[]{:S(2)}) %copy-start.8) | copy-done | bytes 104
  39.2 0.0 copy-start.10
  39.2 0.7 %copy-done.10 = f32[20]{0:T(128)S(1)} copy-done((f32[20]{0:T(128)S(1)}, f32[20]{0:T(128)}, u32[]{:S(2)}) %copy-start.10) | copy-done | bytes 104
  39.9 0.0 copy-start.11
  39.9 1.1 %copy-done.11 = bf16[256,1280]{1,0:T(8,128)(2,1)S(1)} copy-done((bf16[256,1280]{1,0:T(8,128)(2,1)S(1)}, bf16[256,1280]{1,0:T(8,128)(2,1)}, u32[]{:S(2)}) %copy-start.11) | copy-done | bytes 655384
  41.0 0.0 copy-start
  41.0 0.0 copy-start.2
  41.0 0.0 copy-start.4
  41.0 0.0 copy-start.5
  41.0 0.0 copy-start.7
  41.0 0.0 copy-start.9
  41.0 3.4 %shard_map.129.y_ref = f32[256,1280]{1,0:T(8,128)S(1)} custom-call(bf16[256,1280]{1,0:T(8,128)(2,1)S(1)} %copy-done.11, bf16[256,256]{1,0:T(8,128)(2,1)S(1)} %copy-done.1, f32[20,256]{1,0:T(8,128)S(1)} %copy-done.3, f32[1,20]{1,0:T(1,128)S(1)} %bitcast.14, f32[1,20]{1,0:T(1,128)S(1)} %bitcast.17, f32[20]{0:T(128)S(1)} %copy-done.10), custom_call_target="tpu_custom_call" | custom-call | flops 4000000000 | bytes 1048576 | tf_op jit(solution)/shard_map/pallas_call | solution.py:310
  44.4 2.2 %all-to-all-done.1 = bf16[16,8,1280]{2,1,0:T(8,128)(2,1)S(1)} async-done(((bf16[16,8,1280]{2,1,0:T(8,128)(2,1)}), bf16[16,8,1280]{2,1,0:T(8,128)(2,1)S(1)}, u32[]{:S(2)}, u32[]{:S(2)}) %all-to-all-start.1) | async-done | bytes 327712 | tf_op jit(solution)/shard_map/all_to_all | solution.py:316
  46.7 0.0 copy-done
  46.7 0.0 copy-done.2
  46.7 0.0 copy-done.4
  46.7 0.0 copy-done.5
  46.7 0.0 copy-done.7
  46.7 0.0 copy-done.9
  46.7 4.3 %shard_map.130 = (bf16[256,1280]{1,0:T(8,128)(2,1)S(1)}, f32[256,128]{1,0:T(8,128)S(1)}, bf16[256,1408]{1,0:T(8,128)(2,1)S(1)}, bf16[1280,1280]{1,0:T(8,128)(2,1)S(1)}) custom-call(s32[1,1]{1,0:T(1,128)} %bitcast.me_ref, bf16[128,1280]{1,0:T(8,128)(2,1)S(1)} %bitcast.11, bf16[256,256]{1,0:T(8,128)(2,1)S(1)} %copy-done.2, f32[256,1280]{1,0:T(8,128)S(1)} %shard_map.129.y_ref, ...), custom_call_target="tpu_custom_call" | custom-call | flops 2000000000 | bytes 1048576 | tf_op jit(solution)/shard_map/pallas_call | solution.py:320
  51.1 0.1 collective-permute-start.1
  51.1 1.0 %shard_map.131.own_ref = f32[256,1280]{1,0:T(8,128)S(1)} custom-call(bf16[256,1280]{1,0:T(8,128)(2,1)S(1)} %get-tuple-element.15.gated_ref, bf16[1280,1280]{1,0:T(8,128)(2,1)S(1)} %get-tuple-element.16.weight_ref), custom_call_target="tpu_custom_call" | custom-call | flops 2000000000 | bytes 1048576 | tf_op jit(solution)/shard_map/pallas_call | solution.py:337
  52.2 1.2 %collective-permute-done.1.got_ref = bf16[256,1408]{1,0:T(8,128)(2,1)S(1)} collective-permute-done((bf16[256,1408]{1,0:T(8,128)(2,1)S(1)}, bf16[256,1408]{1,0:T(8,128)(2,1)S(1)}, u32[]{:S(2)}, u32[]{:S(2)}) %collective-permute-start.1) | collective-permute-done | bytes 720928 | tf_op jit(solution)/shard_map/ppermute | solution.py:336
  53.3 1.1 %shard_map.132 = bf16[256,1280]{1,0:T(8,128)(2,1)} custom-call(f32[256,1280]{1,0:T(8,128)S(1)} %shard_map.131.own_ref, f32[256,128]{1,0:T(8,128)S(1)} %get-tuple-element.17.squares_ref, bf16[256,1408]{1,0:T(8,128)(2,1)S(1)} %collective-permute-done.1.got_ref), custom_call_target="tpu_custom_call" | custom-call | flops 100000000 | bytes 1048576 | tf_op jit(solution)/shard_map/pallas_call | solution.py:338
  (1 shorter events, 0.0 us)
Async XLA Ops:
  1.4 6.4 %collective-permute-start = (bf16[8,1536]{1,0:T(8,128)(2,1)S(1)}, bf16[8,1536]{1,0:T(8,128)(2,1)S(1)}, u32[]{:S(2)}, u32[]{:S(2)}) collective-permute-start(bf16[8,1536]{1,0:T(8,128)(2,1)S(1)} %pad_maximum_fusion), channel_id=1, source_target_pairs={{0,2},{2,4},{4,6},{6,8},{8,10},{10,12},{12,14},{14,16},{16,18},{18... | collective-permute-start | bytes 73736 | tf_op jit(solution)/shard_map/ppermute | solution.py:277
  7.8 0.6 %copy-start.12 = (bf16[8,1536]{1,0:T(8,128)(2,1)}, bf16[8,1536]{1,0:T(8,128)(2,1)S(1)}, u32[]{:S(2)}) copy-start(bf16[8,1536]{1,0:T(8,128)(2,1)S(1)} %collective-permute-done.refs_0_) | copy-start | bytes 73732
  32.7 14.0 %all-to-all-start.1 = ((bf16[16,8,1280]{2,1,0:T(8,128)(2,1)}), bf16[16,8,1280]{2,1,0:T(8,128)(2,1)S(1)}, u32[]{:S(2)}, u32[]{:S(2)}) async-start(bf16[16,8,1280]{2,1,0:T(8,128)(2,1)} %bitcast.7), calls=%async_computation.1 | async-start | bytes 655360 | tf_op jit(solution)/shard_map/all_to_all | solution.py:316
  36.3 0.9 %copy-start.1 = (bf16[256,256]{1,0:T(8,128)(2,1)S(1)}, bf16[256,256]{1,0:T(8,128)(2,1)}, u32[]{:S(2)}) copy-start(bf16[256,256]{1,0:T(8,128)(2,1)} %get-tuple-element.13.bc_ref) | copy-start | bytes 393220
  37.2 0.7 %copy-start.3 = (f32[20,256]{1,0:T(8,128)S(1)}, f32[20,256]{1,0:T(8,128)}, u32[]{:S(2)}) copy-start(f32[20,256]{1,0:T(8,128)} %raw_ref.3) | copy-start | bytes 61444
  37.9 0.7 %copy-start.6 = (f32[20]{0:T(128)S(1)}, f32[20]{0:T(128)}, u32[]{:S(2)}) copy-start(f32[20]{0:T(128)} %param.21) | copy-start | bytes 244
  38.6 0.7 %copy-start.8 = (f32[20]{0:T(128)S(1)}, f32[20]{0:T(128)}, u32[]{:S(2)}) copy-start(f32[20]{0:T(128)} %param.22) | copy-start | bytes 244
  39.2 0.7 %copy-start.10 = (f32[20]{0:T(128)S(1)}, f32[20]{0:T(128)}, u32[]{:S(2)}) copy-start(f32[20]{0:T(128)} %skip_ref.1) | copy-start | bytes 244
  39.9 1.1 %copy-start.11 = (bf16[256,1280]{1,0:T(8,128)(2,1)S(1)}, bf16[256,1280]{1,0:T(8,128)(2,1)}, u32[]{:S(2)}) copy-start(bf16[256,1280]{1,0:T(8,128)(2,1)} %get-tuple-element.14.x_ref) | copy-start | bytes 1966084
  41.0 5.7 %copy-start = (bf16[256,1280]{1,0:T(8,128)(2,1)S(1)}, bf16[256,1280]{1,0:T(8,128)(2,1)}, u32[]{:S(2)}) copy-start(bf16[256,1280]{1,0:T(8,128)(2,1)} %gate_ref.1) | copy-start | bytes 1966084
  41.0 5.7 %copy-start.2 = (bf16[256,256]{1,0:T(8,128)(2,1)S(1)}, bf16[256,256]{1,0:T(8,128)(2,1)}, u32[]{:S(2)}) copy-start(bf16[256,256]{1,0:T(8,128)(2,1)} %get-tuple-element.13.bc_ref) | copy-start | bytes 393220
  41.0 5.7 %copy-start.4 = (f32[20,256]{1,0:T(8,128)S(1)}, f32[20,256]{1,0:T(8,128)}, u32[]{:S(2)}) copy-start(f32[20,256]{1,0:T(8,128)} %raw_ref.3) | copy-start | bytes 61444
  41.0 5.7 %copy-start.5 = (f32[1280]{0:T(1024)S(1)}, f32[1280]{0:T(1024)}, u32[]{:S(2)}) copy-start(f32[1280]{0:T(1024)} %param.24) | copy-start | bytes 15364
  41.0 5.7 %copy-start.7 = (f32[20]{0:T(128)S(1)}, f32[20]{0:T(128)}, u32[]{:S(2)}) copy-start(f32[20]{0:T(128)} %param.21) | copy-start | bytes 244
  41.0 5.7 %copy-start.9 = (f32[20]{0:T(128)S(1)}, f32[20]{0:T(128)}, u32[]{:S(2)}) copy-start(f32[20]{0:T(128)} %param.22) | copy-start | bytes 244
  51.1 2.3 %collective-permute-start.1 = (bf16[256,1408]{1,0:T(8,128)(2,1)S(1)}, bf16[256,1408]{1,0:T(8,128)(2,1)S(1)}, u32[]{:S(2)}, u32[]{:S(2)}) collective-permute-start(bf16[256,1408]{1,0:T(8,128)(2,1)S(1)} %get-tuple-element.18), channel_id=1, source_target_pairs={{0,1},{1,0},{2,3},{3,2},{4,5},{5,4},{6,7},{7,6},{8,9},{9,8},{10,11... | collective-permute-start | bytes 2162696 | tf_op jit(solution)/shard_map/ppermute | solution.py:336

commit v3 on v2

--- a/solution.py
+++ b/solution.py
@@ -188,17 +188,13 @@
 
 def gate_kernel(
     me_ref, entering_ref, bc_ref, y_ref, raw_ref, step_bias_ref, decay_ref,
-    gate_ref, gain_ref, weight_ref, gated_ref, squares_ref, send_ref, mine_ref,
-    parts, theirs_ref, sems,
+    gate_ref, gain_ref, weight_ref, gated_ref, squares_ref, send_ref,
+    parts, theirs_ref, sem,
 ):
     rows, width = y_ref.shape
-    me = me_ref[0, 0]
-    peer = pl.multiple_of((1 - me) * width, LANES)
-    mine = pl.multiple_of(me * width, LANES)
-    first = pltpu.make_async_copy(weight_ref.at[:, pl.ds(peer, width)], theirs_ref, sems.at[0])
-    second = pltpu.make_async_copy(weight_ref.at[:, pl.ds(mine, width)], mine_ref, sems.at[1])
+    peer = pl.multiple_of((1 - me_ref[0, 0]) * width, LANES)
+    first = pltpu.make_async_copy(weight_ref.at[:, pl.ds(peer, width)], theirs_ref, sem)
     first.start()
-    second.start()
     half = bc_ref.shape[1] // 2
     _, decay = steps(raw_ref, step_bias_ref, decay_ref)
     cum = jnp.exp(dot(decay, lower(rows), ((1,), (1,)), highest))
@@ -229,19 +225,42 @@
     ).astype(bf16)
     first.wait()
     send_ref[:, :width] = dot(gated_ref[...], theirs_ref[...], ((1,), (0,))).astype(bf16)
-    second.wait()
-
-
-def own_kernel(gated_ref, weight_ref, own_ref):
-    own_ref[...] = dot(gated_ref[...], weight_ref[...], ((1,), (0,)))
-
-
-def finish_kernel(inner, own_ref, squares_ref, got_ref, out_ref):
-    width = own_ref.shape[1]
-    other = got_ref[:, width:].astype(f32)
-    total = squares_ref[:, :1] + other[:, :1] + other[:, SPREAD : SPREAD + 1]
-    scale = lax.rsqrt(total / inner + 1e-05)
-    out_ref[...] = ((own_ref[...] + got_ref[:, :width].astype(f32)) * scale).astype(bf16)
+
+
+def own_kernel(me_ref, gated_ref, weight_ref, own_ref, mine_ref, sems):
+    width = gated_ref.shape[1]
+    mine = pl.multiple_of(me_ref[0, 0] * width, LANES)
+    half = width // 2
+    parts = [slice(0, half), slice(half, width)]
+    copies = [
+        pltpu.make_async_copy(
+            weight_ref.at[rows, pl.ds(mine, width)], mine_ref.at[rows, :], sems.at[i]
+        )
+        for i, rows in enumerate(parts)
+    ]
+    for copy in copies:
+        copy.start()
+    copies[0].wait()
+    own_ref[...] = dot(gated_ref[:, parts[0]], mine_ref[parts[0], :], ((1,), (0,)))
+    copies[1].wait()
+    own_ref[...] += dot(gated_ref[:, parts[1]], mine_ref[parts[1], :], ((1,), (0,)))
+
+
+def finish_kernel(inner, own_ref, squares_ref, got_ref, out_ref, kept, sems):
+    height, width = own_ref.shape
+    step = height // 4
+    copies = []
+    for number in range(4):
+        rows = slice(number * step, (number + 1) * step)
+        other = got_ref[rows, width:].astype(f32)
+        total = squares_ref[rows, :1] + other[:, :1] + other[:, SPREAD : SPREAD + 1]
+        scale = lax.rsqrt(total / inner + 1e-05)
+        kept[rows, :] = ((own_ref[rows, :] + got_ref[rows, :width].astype(f32)) * scale).astype(bf16)
+        copy = pltpu.make_async_copy(kept.at[rows, :], out_ref.at[rows, :], sems.at[number])
+        copy.start()
+        copies.append(copy)
+    for copy in copies:
+        copy.wait()
 
 
 VMEM = pl.BlockSpec(memory_space=pltpu.VMEM)
@@ -264,6 +283,7 @@
 
 WHOLE = 67043328
 GATE_LIMIT = 44 << 20
+OWN_LIMIT = 52 << 20
 
 
 def local(
@@ -274,11 +294,9 @@
     states = state_input.shape[1]
     half = states // 2
     devices = lax.axis_size("seq")
-    halo = lax.ppermute(
-        jnp.concatenate([inner_input[rows - 8 :], state_input[rows - 8 :]], axis=1),
-        "seq",
-        [(d, d + 1) for d in range(devices - 1)],
-    )
+    shape = jax.ShapeDtypeStruct
+    edge = jnp.concatenate([inner_input[rows - 8 :], state_input[rows - 8 :]], axis=1)
+    halo = lax.ppermute(edge, "seq", [(d, d + 1) for d in range(devices - 1)])
     step_args = (step_raw, step_bias[None], decay_log[None])
     given = (
         halo, *step_args, conv_state, bias_state.reshape(-1, LANES), state_input,
@@ -317,27 +335,32 @@
         before.reshape(devices, each, width), "seq", split_axis=0, concat_axis=0, tiled=True
     ).reshape(half, width)
     me = lax.axis_index("tp").astype(jnp.int32).reshape(1, 1)
-    gated, squares, send, mine = call(
+    gated, squares, send = call(
         gate_kernel,
         [SMEM] + [VMEM] * 8 + [HBM],
         [
             shape((rows, width), bf16), shape((rows, LANES), f32),
-            shape((rows, width + LANES), bf16), shape((width, width), bf16),
+            shape((rows, width + LANES), bf16),
         ],
         2e9,
         [
             pltpu.VMEM((2 * SPREAD, rows), f32),
             pltpu.VMEM((width, width), bf16),
-            pltpu.SemaphoreType.DMA((2,)),
+            pltpu.SemaphoreType.DMA,
         ],
         GATE_LIMIT,
     )(me, entering, bc, y, *step_args, gate_input, norm_gain.reshape(-1, LANES), out_weight)
     pairs = lax.axis_size("tp")
     other = lax.ppermute(send, "tp", [(d, pairs - 1 - d) for d in range(pairs)])
-    own = call(own_kernel, [VMEM, VMEM], shape((rows, width), f32), 2e9)(gated, mine)
+    own = call(
+        own_kernel, [SMEM, VMEM, HBM], shape((rows, width), f32), 2e9,
+        [pltpu.VMEM((width, width), bf16), pltpu.SemaphoreType.DMA((2,))], OWN_LIMIT,
+    )(me, gated, out_weight)
     return call(
         functools.partial(finish_kernel, float(width * pairs)),
         [VMEM] * 3, shape((rows, width), bf16), 1e8,
+        [pltpu.VMEM((rows, width), bf16), pltpu.SemaphoreType.DMA((4,))],
+        out=HBM,
     )(own, squares, other)
 
 

time: 55 us -> 55.6 us (1.011)
  local copies, waits for them, and re-layouts: 6.73 us -> 2.06 us
  waiting for transfers between devices: 4.89 us -> 8.3 us
  Pallas kernels: 15.7 us -> 17.4 us
    unnamed x26 -> x18, local copies, waits for them, and re-layouts: 5.31 us -> 0.64 us
    all_to_all x1, waiting for transfers between devices: 2.23 us -> 6.8 us  [local(): lax.all_to_all(before.reshape(devices, each, width), 'seq', split_axis=0,...]
    pallas_call x1, Pallas kernels: 1.01 us -> 2.77 us  [local(): call(own_kernel, [SMEM, VMEM, HBM], shape((rows, width), f32), 2000000000...]
    ppermute x1, waiting for transfers between devices: 1.16 us -> 0.01 us  [local(): other = lax.ppermute(send, 'tp', [(d, pairs - 1 - d) for d in range(pairs)])]
  transfers between devices with their start and end apart: 3 -> 3, of which waited for: 3 -> 2; matrix products, arithmetic and copies ran while one was open for 0% -> 0% of each run, Pallas kernels for 8% -> 11%
where the time goes in v3:
time: 55.6 us; the launch traced here: 55.1 us
  blocking collectives  18.6 us (33%)
  Pallas kernels  17.4 us (31%)
  starting transfers between devices  8.5 us (15%)
  waiting for transfers between devices  8.3 us (15%)
  local copies, waits for them, and re-layouts  2.06 us (4%)
    all_to_all x1, blocking collectives, local(): lax.all_to_all(payload.reshape(devices, each, width + LANES), 'seq', spli...  18.6 us
    all_to_all x1, waiting for transfers between devices, local(): lax.all_to_all(before.reshape(devices, each, width), 'seq', split_axis=0,...  6.8 us
    ppermute x1, starting transfers between devices, local(): halo = lax.ppermute(edge, 'seq', [(d, d + 1) for d in range(devices - 1)])  4.86 us
    pallas_call x1, Pallas kernels, local(): call(functools.partial(update_kernel, len(given)), [HBM] * len(given), [s...  4.83 us
    pallas_call x1, Pallas kernels, local(): call(gate_kernel, [SMEM] + [VMEM] * 8 + [HBM], [shape((rows, width), bf16...  4.34 us
    all_to_all x1, starting transfers between devices, local(): lax.all_to_all(before.reshape(devices, each, width), 'seq', split_axis=0,...  3.56 us
    pallas_call x1, Pallas kernels, local(): call(inside_kernel, [VMEM] * 5 + [SMEM], shape((rows, width), f32), 40000...  3.5 us
    pallas_call x1, Pallas kernels, local(): call(own_kernel, [SMEM, VMEM, HBM], shape((rows, width), f32), 2000000000...  2.77 us
  transfers between devices with their start and end apart: 3, of which 2 were waited for; matrix products, arithmetic and copies ran while one was open for 0% of the time, Pallas kernels for 11%

profile of v3, /device:TPU:0, one launch (start us, length us, event | category | flops | bytes accessed | tf_op | source)
XLA Modules:
  0.0 55.1 jit_solution(2469967148788674985)
XLA Ops:
  0.0 0.7 %slice.7 = bf16[8,256]{1,0:T(8,128)(2,1)S(1)} slice(bf16[256,256]{1,0:T(8,128)(2,1)} %refs_6_.1), slice={[248:256], [0:256]} | slice | bytes 8192 | tf_op jit(solution)/shard_map/slice | solution.py:298
  0.7 0.7 %slice.6 = bf16[8,1280]{1,0:T(8,128)(2,1)S(1)} slice(bf16[256,1280]{1,0:T(8,128)(2,1)} %refs_9_.1), slice={[248:256], [0:1280]} | slice | bytes 40960 | tf_op jit(solution)/shard_map/slice | solution.py:298
  1.4 4.9 %collective-permute-start = (bf16[8,1536]{1,0:T(8,128)(2,1)S(1)}, bf16[8,1536]{1,0:T(8,128)(2,1)S(1)}, u32[]{:S(2)}, u32[]{:S(2)}) collective-permute-start(bf16[8,1536]{1,0:T(8,128)(2,1)S(1)} %pad_maximum_fusion), channel_id=1, source_target_pairs={{0,2},{2,4},{4,6},{6,8},{8,10},{10,12},{12,14},{14,16},{16,18},{18... | collective-permute-start | bytes 73736 | tf_op jit(solution)/shard_map/ppermute | solution.py:299
  6.3 1.5 %collective-permute-done.refs_0_ = bf16[8,1536]{1,0:T(8,128)(2,1)S(1)} collective-permute-done((bf16[8,1536]{1,0:T(8,128)(2,1)S(1)}, bf16[8,1536]{1,0:T(8,128)(2,1)S(1)}, u32[]{:S(2)}, u32[]{:S(2)}) %collective-permute-start) | collective-permute-done | bytes 24608 | tf_op jit(solution)/shard_map/ppermute | solution.py:299
  7.8 0.0 copy-start.8
  7.8 0.6 %copy-done.8 = bf16[8,1536]{1,0:T(8,128)(2,1)} copy-done((bf16[8,1536]{1,0:T(8,128)(2,1)}, bf16[8,1536]{1,0:T(8,128)(2,1)S(1)}, u32[]{:S(2)}) %copy-start.8) | copy-done | bytes 24600
  8.4 4.8 %shard_map.127 = (bf16[256,1280]{1,0:T(8,128)(2,1)}, bf16[256,256]{1,0:T(8,128)(2,1)}, bf16[128,1408]{1,0:T(8,128)(2,1)}) custom-call(bf16[8,1536]{1,0:T(8,128)(2,1)} %copy-done.8, f32[20,256]{1,0:T(8,128)} %raw_ref.3, f32[1,20]{1,0:T(1,128)} %bitcast.13, f32[1,20]{1,0:T(1,128)} %bitcast.16, f32[4,256]{1,0:T(4,128)} %refs_4_.1, f32[2,128]{1,0:T(2,128)} %bitcast.21, ...), custom_call_target="tpu_custom_call" | custom-call | flops 2000000000 | bytes 1048576 | tf_op jit(solution)/shard_map/pallas_call | solution.py:307
  13.2 0.0 copy-start.1
  13.2 0.0 copy-start.2
  13.2 0.0 copy-start.4
  13.3 0.0 copy-start.5
  13.3 0.0 copy-start.6
  13.3 0.0 copy-start.7
  13.3 18.6 %all_to_all.10 = bf16[16,8,1408]{2,1,0:T(8,128)(2,1)S(1)} all-to-all(bf16[16,8,1408]{2,1,0:T(8,128)(2,1)} %bitcast.19), channel_id=1, replica_groups=mesh['seq'=16,'tp'=2] {'seq'}, dimensions={0} | all-to-all | bytes 720896 | tf_op jit(solution)/shard_map/all_to_all | solution.py:325
  31.9 1.0 %shard_map.128 = bf16[128,1280]{1,0:T(8,128)(2,1)} custom-call(bf16[128,1408]{1,0:T(8,128)(2,1)S(1)} %bitcast.10), custom_call_target="tpu_custom_call" | custom-call | flops 100000000 | bytes 1048576 | tf_op jit(solution)/shard_map/pallas_call | solution.py:331
  32.9 3.6 %all-to-all-start.1 = ((bf16[16,8,1280]{2,1,0:T(8,128)(2,1)}), bf16[16,8,1280]{2,1,0:T(8,128)(2,1)S(1)}, u32[]{:S(2)}, u32[]{:S(2)}) async-start(bf16[16,8,1280]{2,1,0:T(8,128)(2,1)} %bitcast.7), calls=%async_computation.1 | async-start | bytes 655360 | tf_op jit(solution)/shard_map/all_to_all | solution.py:334
  36.5 0.0 copy-done.1
  36.5 0.0 copy-done.2
  36.5 0.0 copy-done.4
  36.5 0.0 copy-done.5
  36.5 0.0 copy-done.6
  36.5 0.0 copy-done.7
  36.5 0.0 copy-start
  36.5 0.0 copy-start.3
  36.6 3.5 %shard_map.129.y_ref = f32[256,1280]{1,0:T(8,128)S(1)} custom-call(bf16[256,1280]{1,0:T(8,128)(2,1)S(1)} %copy-done.7, bf16[256,256]{1,0:T(8,128)(2,1)S(1)} %copy-done.1, f32[20,256]{1,0:T(8,128)S(1)} %copy-done.2, f32[1,20]{1,0:T(1,128)S(1)} %bitcast.14, f32[1,20]{1,0:T(1,128)S(1)} %bitcast.17, f32[20]{0:T(128)S(1)} %copy-done.6), custom_call_target="tpu_custom_call" | custom-call | flops 4000000000 | bytes 1048576 | tf_op jit(solution)/shard_map/pallas_call | solution.py:328
  40.1 6.8 %all-to-all-done.1 = bf16[16,8,1280]{2,1,0:T(8,128)(2,1)S(1)} async-done(((bf16[16,8,1280]{2,1,0:T(8,128)(2,1)}), bf16[16,8,1280]{2,1,0:T(8,128)(2,1)S(1)}, u32[]{:S(2)}, u32[]{:S(2)}) %all-to-all-start.1) | async-done | bytes 327712 | tf_op jit(solution)/shard_map/all_to_all | solution.py:334
  46.9 0.0 copy-done
  46.9 0.0 copy-done.3
  46.9 4.3 %shard_map.130 = (bf16[256,1280]{1,0:T(8,128)(2,1)S(1)}, f32[256,128]{1,0:T(8,128)S(1)}, bf16[256,1408]{1,0:T(8,128)(2,1)S(1)}) custom-call(s32[1,1]{1,0:T(1,128)} %bitcast.me_ref, bf16[128,1280]{1,0:T(8,128)(2,1)S(1)} %bitcast.11, bf16[256,256]{1,0:T(8,128)(2,1)S(1)} %copy-done.1, f32[256,1280]{1,0:T(8,128)S(1)} %shard_map.129.y_ref, ...), custom_call_target="tpu_custom_call" | custom-call | flops 2000000000 | bytes 1048576 | tf_op jit(solution)/shard_map/pallas_call | solution.py:338
  51.2 0.1 collective-permute-start.1
  51.3 2.8 %shard_map.131.own_ref = f32[256,1280]{1,0:T(8,128)S(1)} custom-call(s32[1,1]{1,0:T(1,128)} %bitcast.me_ref, bf16[256,1280]{1,0:T(8,128)(2,1)S(1)} %get-tuple-element.14.gated_ref, bf16[1280,2560]{1,0:T(8,128)(2,1)} %weight_ref.3), custom_call_target="tpu_custom_call" | custom-call | flops 2000000000 | bytes 1048576 | tf_op jit(solution)/shard_map/pallas_call | solution.py:355
  54.1 0.0 collective-permute-done.1.got_ref
  54.1 1.0 %shard_map.132 = bf16[256,1280]{1,0:T(8,128)(2,1)} custom-call(f32[256,1280]{1,0:T(8,128)S(1)} %shard_map.131.own_ref, f32[256,128]{1,0:T(8,128)S(1)} %get-tuple-element.15.squares_ref, bf16[256,1408]{1,0:T(8,128)(2,1)S(1)} %collective-permute-done.1.got_ref), custom_call_target="tpu_custom_call" | custom-call | flops 100000000 | bytes 1048576 | tf_op jit(solution)/shard_map/pallas_call | solution.py:359
  (1 shorter events, 0.0 us)
Async XLA Ops:
  1.4 6.4 %collective-permute-start = (bf16[8,1536]{1,0:T(8,128)(2,1)S(1)}, bf16[8,1536]{1,0:T(8,128)(2,1)S(1)}, u32[]{:S(2)}, u32[]{:S(2)}) collective-permute-start(bf16[8,1536]{1,0:T(8,128)(2,1)S(1)} %pad_maximum_fusion), channel_id=1, source_target_pairs={{0,2},{2,4},{4,6},{6,8},{8,10},{10,12},{12,14},{14,16},{16,18},{18... | collective-permute-start | bytes 73736 | tf_op jit(solution)/shard_map/ppermute | solution.py:299
  7.8 0.6 %copy-start.8 = (bf16[8,1536]{1,0:T(8,128)(2,1)}, bf16[8,1536]{1,0:T(8,128)(2,1)S(1)}, u32[]{:S(2)}) copy-start(bf16[8,1536]{1,0:T(8,128)(2,1)S(1)} %collective-permute-done.refs_0_) | copy-start | bytes 73732
  13.2 23.2 %copy-start.1 = (bf16[256,256]{1,0:T(8,128)(2,1)S(1)}, bf16[256,256]{1,0:T(8,128)(2,1)}, u32[]{:S(2)}) copy-start(bf16[256,256]{1,0:T(8,128)(2,1)} %get-tuple-element.12.bc_ref) | copy-start | bytes 393220
  13.2 23.2 %copy-start.2 = (f32[20,256]{1,0:T(8,128)S(1)}, f32[20,256]{1,0:T(8,128)}, u32[]{:S(2)}) copy-start(f32[20,256]{1,0:T(8,128)} %raw_ref.3) | copy-start | bytes 61444
  13.2 23.2 %copy-start.4 = (f32[20]{0:T(128)S(1)}, f32[20]{0:T(128)}, u32[]{:S(2)}) copy-start(f32[20]{0:T(128)} %param.21) | copy-start | bytes 244
  13.3 23.2 %copy-start.5 = (f32[20]{0:T(128)S(1)}, f32[20]{0:T(128)}, u32[]{:S(2)}) copy-start(f32[20]{0:T(128)} %param.22) | copy-start | bytes 244
  13.3 23.2 %copy-start.6 = (f32[20]{0:T(128)S(1)}, f32[20]{0:T(128)}, u32[]{:S(2)}) copy-start(f32[20]{0:T(128)} %skip_ref.1) | copy-start | bytes 244
  13.3 23.2 %copy-start.7 = (bf16[256,1280]{1,0:T(8,128)(2,1)S(1)}, bf16[256,1280]{1,0:T(8,128)(2,1)}, u32[]{:S(2)}) copy-start(bf16[256,1280]{1,0:T(8,128)(2,1)} %get-tuple-element.13.x_ref) | copy-start | bytes 1966084
  32.9 14.0 %all-to-all-start.1 = ((bf16[16,8,1280]{2,1,0:T(8,128)(2,1)}), bf16[16,8,1280]{2,1,0:T(8,128)(2,1)S(1)}, u32[]{:S(2)}, u32[]{:S(2)}) async-start(bf16[16,8,1280]{2,1,0:T(8,128)(2,1)} %bitcast.7), calls=%async_computation.1 | async-start | bytes 655360 | tf_op jit(solution)/shard_map/all_to_all | solution.py:334
  36.5 10.3 %copy-start = (bf16[256,1280]{1,0:T(8,128)(2,1)S(1)}, bf16[256,1280]{1,0:T(8,128)(2,1)}, u32[]{:S(2)}) copy-start(bf16[256,1280]{1,0:T(8,128)(2,1)} %gate_ref.1) | copy-start | bytes 1966084
  36.5 10.3 %copy-start.3 = (f32[1280]{0:T(1024)S(1)}, f32[1280]{0:T(1024)}, u32[]{:S(2)}) copy-start(f32[1280]{0:T(1024)} %param.24) | copy-start | bytes 15364
  51.2 2.9 %collective-permute-start.1 = (bf16[256,1408]{1,0:T(8,128)(2,1)S(1)}, bf16[256,1408]{1,0:T(8,128)(2,1)S(1)}, u32[]{:S(2)}, u32[]{:S(2)}) collective-permute-start(bf16[256,1408]{1,0:T(8,128)(2,1)S(1)} %get-tuple-element.16), channel_id=1, source_target_pairs={{0,1},{1,0},{2,3},{3,2},{4,5},{5,4},{6,7},{7,6},{8,9},{9,8},{10,11... | collective-permute-start | bytes 2162696 | tf_op jit(solution)/shard_map/ppermute | solution.py:354

commit v4 on v3

--- a/solution.py
+++ b/solution.py
@@ -193,8 +193,14 @@
 ):
     rows, width = y_ref.shape
     peer = pl.multiple_of((1 - me_ref[0, 0]) * width, LANES)
-    first = pltpu.make_async_copy(weight_ref.at[:, pl.ds(peer, width)], theirs_ref, sem)
-    first.start()
+    step = width // 8
+    pieces = [slice(i * step, (i + 1) * step) for i in range(8)]
+    copies = [
+        pltpu.make_async_copy(weight_ref.at[p, pl.ds(peer, width)], theirs_ref.at[p, :], sem.at[i])
+        for i, p in enumerate(pieces)
+    ]
+    for copy in copies:
+        copy.start()
     half = bc_ref.shape[1] // 2
     _, decay = steps(raw_ref, step_bias_ref, decay_ref)
     cum = jnp.exp(dot(decay, lower(rows), ((1,), (1,)), highest))
@@ -223,7 +229,8 @@
         jnp.broadcast_to(high.astype(f32), (rows, LANES)),
         jnp.broadcast_to(low.astype(f32), (rows, LANES)),
     ).astype(bf16)
-    first.wait()
+    for copy in copies:
+        copy.wait()
     send_ref[:, :width] = dot(gated_ref[...], theirs_ref[...], ((1,), (0,))).astype(bf16)
 
 
@@ -231,7 +238,8 @@
     width = gated_ref.shape[1]
     mine = pl.multiple_of(me_ref[0, 0] * width, LANES)
     half = width // 2
-    parts = [slice(0, half), slice(half, width)]
+    step = width // 8
+    parts = [slice(i * step, (i + 1) * step) for i in range(8)]
     copies = [
         pltpu.make_async_copy(
             weight_ref.at[rows, pl.ds(mine, width)], mine_ref.at[rows, :], sems.at[i]
@@ -240,10 +248,12 @@
     ]
     for copy in copies:
         copy.start()
-    copies[0].wait()
-    own_ref[...] = dot(gated_ref[:, parts[0]], mine_ref[parts[0], :], ((1,), (0,)))
-    copies[1].wait()
-    own_ref[...] += dot(gated_ref[:, parts[1]], mine_ref[parts[1], :], ((1,), (0,)))
+    for copy in copies[:4]:
+        copy.wait()
+    own_ref[...] = dot(gated_ref[:, :half], mine_ref[:half, :], ((1,), (0,)))
+    for copy in copies[4:]:
+        copy.wait()
+    own_ref[...] += dot(gated_ref[:, half:], mine_ref[half:, :], ((1,), (0,)))
 
 
 def finish_kernel(inner, own_ref, squares_ref, got_ref, out_ref, kept, sems):
@@ -346,7 +356,7 @@
         [
             pltpu.VMEM((2 * SPREAD, rows), f32),
             pltpu.VMEM((width, width), bf16),
-            pltpu.SemaphoreType.DMA,
+            pltpu.SemaphoreType.DMA((8,)),
         ],
         GATE_LIMIT,
     )(me, entering, bc, y, *step_args, gate_input, norm_gain.reshape(-1, LANES), out_weight)
@@ -354,7 +364,7 @@
     other = lax.ppermute(send, "tp", [(d, pairs - 1 - d) for d in range(pairs)])
     own = call(
         own_kernel, [SMEM, VMEM, HBM], shape((rows, width), f32), 2e9,
-        [pltpu.VMEM((width, width), bf16), pltpu.SemaphoreType.DMA((2,))], OWN_LIMIT,
+        [pltpu.VMEM((width, width), bf16), pltpu.SemaphoreType.DMA((8,))], OWN_LIMIT,
     )(me, gated, out_weight)
     return call(
         functools.partial(finish_kernel, float(width * pairs)),

time: 55.6 us -> 55.6 us (level)
  no operation moved by 1% of the time
where the time goes in v4:
time: 55.6 us; the launch traced here: 55.1 us
  blocking collectives  18.6 us (33%)
  Pallas kernels  17.5 us (31%)
  starting transfers between devices  8.5 us (15%)
  waiting for transfers between devices  8.3 us (15%)
  local copies, waits for them, and re-layouts  2.06 us (4%)
    all_to_all x1, blocking collectives, local(): lax.all_to_all(payload.reshape(devices, each, width + LANES), 'seq', spli...  18.6 us
    all_to_all x1, waiting for transfers between devices, local(): lax.all_to_all(before.reshape(devices, each, width), 'seq', split_axis=0,...  6.8 us
    ppermute x1, starting transfers between devices, local(): halo = lax.ppermute(edge, 'seq', [(d, d + 1) for d in range(devices - 1)])  4.86 us
    pallas_call x1, Pallas kernels, local(): call(functools.partial(update_kernel, len(given)), [HBM] * len(given), [s...  4.83 us
    pallas_call x1, Pallas kernels, local(): call(gate_kernel, [SMEM] + [VMEM] * 8 + [HBM], [shape((rows, width), bf16...  4.36 us
    all_to_all x1, starting transfers between devices, local(): lax.all_to_all(before.reshape(devices, each, width), 'seq', split_axis=0,...  3.56 us
    pallas_call x1, Pallas kernels, local(): call(inside_kernel, [VMEM] * 5 + [SMEM], shape((rows, width), f32), 40000...  3.5 us
    pallas_call x1, Pallas kernels, local(): call(own_kernel, [SMEM, VMEM, HBM], shape((rows, width), f32), 2000000000...  2.77 us
  transfers between devices with their start and end apart: 3, of which 2 were waited for; matrix products, arithmetic and copies ran while one was open for 0% of the time, Pallas kernels for 11%

profile of v4, /device:TPU:0, one launch (start us, length us, event | category | flops | bytes accessed | tf_op | source)
XLA Modules:
  0.0 55.1 jit_solution(6395424358530912591)
XLA Ops:
  0.0 0.7 %slice.7 = bf16[8,256]{1,0:T(8,128)(2,1)S(1)} slice(bf16[256,256]{1,0:T(8,128)(2,1)} %refs_6_.1), slice={[248:256], [0:256]} | slice | bytes 8192 | tf_op jit(solution)/shard_map/slice | solution.py:308
  0.7 0.7 %slice.6 = bf16[8,1280]{1,0:T(8,128)(2,1)S(1)} slice(bf16[256,1280]{1,0:T(8,128)(2,1)} %refs_9_.1), slice={[248:256], [0:1280]} | slice | bytes 40960 | tf_op jit(solution)/shard_map/slice | solution.py:308
  1.4 4.9 %collective-permute-start = (bf16[8,1536]{1,0:T(8,128)(2,1)S(1)}, bf16[8,1536]{1,0:T(8,128)(2,1)S(1)}, u32[]{:S(2)}, u32[]{:S(2)}) collective-permute-start(bf16[8,1536]{1,0:T(8,128)(2,1)S(1)} %pad_maximum_fusion), channel_id=1, source_target_pairs={{0,2},{2,4},{4,6},{6,8},{8,10},{10,12},{12,14},{14,16},{16,18},{18... | collective-permute-start | bytes 73736 | tf_op jit(solution)/shard_map/ppermute | solution.py:309
  6.3 1.5 %collective-permute-done.refs_0_ = bf16[8,1536]{1,0:T(8,128)(2,1)S(1)} collective-permute-done((bf16[8,1536]{1,0:T(8,128)(2,1)S(1)}, bf16[8,1536]{1,0:T(8,128)(2,1)S(1)}, u32[]{:S(2)}, u32[]{:S(2)}) %collective-permute-start) | collective-permute-done | bytes 24608 | tf_op jit(solution)/shard_map/ppermute | solution.py:309
  7.8 0.0 copy-start.8
  7.8 0.6 %copy-done.8 = bf16[8,1536]{1,0:T(8,128)(2,1)} copy-done((bf16[8,1536]{1,0:T(8,128)(2,1)}, bf16[8,1536]{1,0:T(8,128)(2,1)S(1)}, u32[]{:S(2)}) %copy-start.8) | copy-done | bytes 24600
  8.4 4.8 %shard_map.127 = (bf16[256,1280]{1,0:T(8,128)(2,1)}, bf16[256,256]{1,0:T(8,128)(2,1)}, bf16[128,1408]{1,0:T(8,128)(2,1)}) custom-call(bf16[8,1536]{1,0:T(8,128)(2,1)} %copy-done.8, f32[20,256]{1,0:T(8,128)} %raw_ref.3, f32[1,20]{1,0:T(1,128)} %bitcast.13, f32[1,20]{1,0:T(1,128)} %bitcast.16, f32[4,256]{1,0:T(4,128)} %refs_4_.1, f32[2,128]{1,0:T(2,128)} %bitcast.21, ...), custom_call_target="tpu_custom_call" | custom-call | flops 2000000000 | bytes 1048576 | tf_op jit(solution)/shard_map/pallas_call | solution.py:317
  13.2 0.0 copy-start.1
  13.2 0.0 copy-start.2
  13.2 0.0 copy-start.4
  13.3 0.0 copy-start.5
  13.3 0.0 copy-start.6
  13.3 0.0 copy-start.7
  13.3 18.6 %all_to_all.10 = bf16[16,8,1408]{2,1,0:T(8,128)(2,1)S(1)} all-to-all(bf16[16,8,1408]{2,1,0:T(8,128)(2,1)} %bitcast.19), channel_id=1, replica_groups=mesh['seq'=16,'tp'=2] {'seq'}, dimensions={0} | all-to-all | bytes 720896 | tf_op jit(solution)/shard_map/all_to_all | solution.py:335
  31.9 1.0 %shard_map.128 = bf16[128,1280]{1,0:T(8,128)(2,1)} custom-call(bf16[128,1408]{1,0:T(8,128)(2,1)S(1)} %bitcast.10), custom_call_target="tpu_custom_call" | custom-call | flops 100000000 | bytes 1048576 | tf_op jit(solution)/shard_map/pallas_call | solution.py:341
  32.9 3.6 %all-to-all-start.1 = ((bf16[16,8,1280]{2,1,0:T(8,128)(2,1)}), bf16[16,8,1280]{2,1,0:T(8,128)(2,1)S(1)}, u32[]{:S(2)}, u32[]{:S(2)}) async-start(bf16[16,8,1280]{2,1,0:T(8,128)(2,1)} %bitcast.7), calls=%async_computation.1 | async-start | bytes 655360 | tf_op jit(solution)/shard_map/all_to_all | solution.py:344
  36.5 0.0 copy-done.1
  36.5 0.0 copy-done.2
  36.5 0.0 copy-done.4
  36.5 0.0 copy-done.5
  36.5 0.0 copy-done.6
  36.5 0.0 copy-done.7
  36.5 0.0 copy-start
  36.5 0.0 copy-start.3
  36.6 3.5 %shard_map.129.y_ref = f32[256,1280]{1,0:T(8,128)S(1)} custom-call(bf16[256,1280]{1,0:T(8,128)(2,1)S(1)} %copy-done.7, bf16[256,256]{1,0:T(8,128)(2,1)S(1)} %copy-done.1, f32[20,256]{1,0:T(8,128)S(1)} %copy-done.2, f32[1,20]{1,0:T(1,128)S(1)} %bitcast.14, f32[1,20]{1,0:T(1,128)S(1)} %bitcast.17, f32[20]{0:T(128)S(1)} %copy-done.6), custom_call_target="tpu_custom_call" | custom-call | flops 4000000000 | bytes 1048576 | tf_op jit(solution)/shard_map/pallas_call | solution.py:338
  40.1 6.8 %all-to-all-done.1 = bf16[16,8,1280]{2,1,0:T(8,128)(2,1)S(1)} async-done(((bf16[16,8,1280]{2,1,0:T(8,128)(2,1)}), bf16[16,8,1280]{2,1,0:T(8,128)(2,1)S(1)}, u32[]{:S(2)}, u32[]{:S(2)}) %all-to-all-start.1) | async-done | bytes 327712 | tf_op jit(solution)/shard_map/all_to_all | solution.py:344
  46.9 0.0 copy-done
  46.9 0.0 copy-done.3
  46.9 4.4 %shard_map.130 = (bf16[256,1280]{1,0:T(8,128)(2,1)S(1)}, f32[256,128]{1,0:T(8,128)S(1)}, bf16[256,1408]{1,0:T(8,128)(2,1)S(1)}) custom-call(s32[1,1]{1,0:T(1,128)} %bitcast.me_ref, bf16[128,1280]{1,0:T(8,128)(2,1)S(1)} %bitcast.11, bf16[256,256]{1,0:T(8,128)(2,1)S(1)} %copy-done.1, f32[256,1280]{1,0:T(8,128)S(1)} %shard_map.129.y_ref, ...), custom_call_target="tpu_custom_call" | custom-call | flops 2000000000 | bytes 1048576 | tf_op jit(solution)/shard_map/pallas_call | solution.py:348
  51.2 0.1 collective-permute-start.1
  51.3 2.8 %shard_map.131.own_ref = f32[256,1280]{1,0:T(8,128)S(1)} custom-call(s32[1,1]{1,0:T(1,128)} %bitcast.me_ref, bf16[256,1280]{1,0:T(8,128)(2,1)S(1)} %get-tuple-element.14.gated_ref, bf16[1280,2560]{1,0:T(8,128)(2,1)} %weight_ref.3), custom_call_target="tpu_custom_call" | custom-call | flops 2000000000 | bytes 1048576 | tf_op jit(solution)/shard_map/pallas_call | solution.py:365
  54.1 0.0 collective-permute-done.1.got_ref
  54.1 1.0 %shard_map.132 = bf16[256,1280]{1,0:T(8,128)(2,1)} custom-call(f32[256,1280]{1,0:T(8,128)S(1)} %shard_map.131.own_ref, f32[256,128]{1,0:T(8,128)S(1)} %get-tuple-element.15.squares_ref, bf16[256,1408]{1,0:T(8,128)(2,1)S(1)} %collective-permute-done.1.got_ref), custom_call_target="tpu_custom_call" | custom-call | flops 100000000 | bytes 1048576 | tf_op jit(solution)/shard_map/pallas_call | solution.py:369
  (1 shorter events, 0.0 us)
Async XLA Ops:
  1.4 6.4 %collective-permute-start = (bf16[8,1536]{1,0:T(8,128)(2,1)S(1)}, bf16[8,1536]{1,0:T(8,128)(2,1)S(1)}, u32[]{:S(2)}, u32[]{:S(2)}) collective-permute-start(bf16[8,1536]{1,0:T(8,128)(2,1)S(1)} %pad_maximum_fusion), channel_id=1, source_target_pairs={{0,2},{2,4},{4,6},{6,8},{8,10},{10,12},{12,14},{14,16},{16,18},{18... | collective-permute-start | bytes 73736 | tf_op jit(solution)/shard_map/ppermute | solution.py:309
  7.8 0.6 %copy-start.8 = (bf16[8,1536]{1,0:T(8,128)(2,1)}, bf16[8,1536]{1,0:T(8,128)(2,1)S(1)}, u32[]{:S(2)}) copy-start(bf16[8,1536]{1,0:T(8,128)(2,1)S(1)} %collective-permute-done.refs_0_) | copy-start | bytes 73732
  13.2 23.2 %copy-start.1 = (bf16[256,256]{1,0:T(8,128)(2,1)S(1)}, bf16[256,256]{1,0:T(8,128)(2,1)}, u32[]{:S(2)}) copy-start(bf16[256,256]{1,0:T(8,128)(2,1)} %get-tuple-element.12.bc_ref) | copy-start | bytes 393220
  13.2 23.2 %copy-start.2 = (f32[20,256]{1,0:T(8,128)S(1)}, f32[20,256]{1,0:T(8,128)}, u32[]{:S(2)}) copy-start(f32[20,256]{1,0:T(8,128)} %raw_ref.3) | copy-start | bytes 61444
  13.2 23.2 %copy-start.4 = (f32[20]{0:T(128)S(1)}, f32[20]{0:T(128)}, u32[]{:S(2)}) copy-start(f32[20]{0:T(128)} %param.21) | copy-start | bytes 244
  13.3 23.2 %copy-start.5 = (f32[20]{0:T(128)S(1)}, f32[20]{0:T(128)}, u32[]{:S(2)}) copy-start(f32[20]{0:T(128)} %param.22) | copy-start | bytes 244
  13.3 23.2 %copy-start.6 = (f32[20]{0:T(128)S(1)}, f32[20]{0:T(128)}, u32[]{:S(2)}) copy-start(f32[20]{0:T(128)} %skip_ref.1) | copy-start | bytes 244
  13.3 23.2 %copy-start.7 = (bf16[256,1280]{1,0:T(8,128)(2,1)S(1)}, bf16[256,1280]{1,0:T(8,128)(2,1)}, u32[]{:S(2)}) copy-start(bf16[256,1280]{1,0:T(8,128)(2,1)} %get-tuple-element.13.x_ref) | copy-start | bytes 1966084
  32.9 14.0 %all-to-all-start.1 = ((bf16[16,8,1280]{2,1,0:T(8,128)(2,1)}), bf16[16,8,1280]{2,1,0:T(8,128)(2,1)S(1)}, u32[]{:S(2)}, u32[]{:S(2)}) async-start(bf16[16,8,1280]{2,1,0:T(8,128)(2,1)} %bitcast.7), calls=%async_computation.1 | async-start | bytes 655360 | tf_op jit(solution)/shard_map/all_to_all | solution.py:344
  36.5 10.3 %copy-start = (bf16[256,1280]{1,0:T(8,128)(2,1)S(1)}, bf16[256,1280]{1,0:T(8,128)(2,1)}, u32[]{:S(2)}) copy-start(bf16[256,1280]{1,0:T(8,128)(2,1)} %gate_ref.1) | copy-start | bytes 1966084
  36.5 10.3 %copy-start.3 = (f32[1280]{0:T(1024)S(1)}, f32[1280]{0:T(1024)}, u32[]{:S(2)}) copy-start(f32[1280]{0:T(1024)} %param.24) | copy-start | bytes 15364
  51.2 2.9 %collective-permute-start.1 = (bf16[256,1408]{1,0:T(8,128)(2,1)S(1)}, bf16[256,1408]{1,0:T(8,128)(2,1)S(1)}, u32[]{:S(2)}, u32[]{:S(2)}) collective-permute-start(bf16[256,1408]{1,0:T(8,128)(2,1)S(1)} %get-tuple-element.16), channel_id=1, source_target_pairs={{0,1},{1,0},{2,3},{3,2},{4,5},{5,4},{6,7},{7,6},{8,9},{9,8},{10,11... | collective-permute-start | bytes 2162696 | tf_op jit(solution)/shard_map/ppermute | solution.py:364
